TPU v7x, 8 devices: a whole 2x2x1 slice. The times are simulated.
8 devices in a mesh: data: 4 (over z, y, x), stage: 2 (over core).
Axes of the slice: x: 2, y: 2, z: 1, core: 2. Of those that a mesh axis runs over, the one named last changes fastest.
Arguments:
- x_in: bfloat16 [4, 64, 8, 2048], P(None, 'data')
- g_out: bfloat16 [4, 64, 8, 2048], P(None, 'data')
- w_gate: bfloat16 [2, 2, 2048, 5632], P('stage', None, 'data')
- w_in: bfloat16 [2, 2, 2048, 5632], P('stage', None, 'data')
- w_out: bfloat16 [2, 2, 5632, 2048], P('stage', None, 'data')
Outputs:
- output 1: bfloat16 [4, 64, 8, 2048], P(None, 'data')
- output 2: float32 [2, 2, 2048, 5632], P('stage', None, 'data')
- output 3: float32 [2, 2, 2048, 5632], P('stage', None, 'data')
- output 4: float32 [2, 2, 5632, 2048], P('stage', None, 'data')
All inputs are finite; a program needn't handle non-finite values.
Results may differ from a plain program's by a relative error of at most 0.0184203.
Values are sent between devices in bfloat16 or wider.
A program may use at most 1 GiB of HBM per device.

v0:
```python
import jax
import jax.numpy as jnp
from jax import lax
from jax.sharding import PartitionSpec as P, NamedSharding

EPS = 1e-6


def contract(left_op, right_op, left_dim, right_dim):
    return lax.dot_general(left_op, right_op, (((left_dim,), (right_dim,)), ((), ())), preferred_element_type=jnp.float32)


def rms_parts(h_rows):
    h_f32 = h_rows.astype(jnp.float32)
    inv_rms = lax.rsqrt(jnp.mean(h_f32 * h_f32, axis=-1, keepdims=True) + EPS)
    return h_f32 * inv_rms, inv_rms


def layer_forward(h_rows, gate_w, in_w, out_w):
    normed_f, inv_rms = rms_parts(h_rows)
    normed = normed_f.astype(jnp.bfloat16)
    gate_pre = jnp.dot(normed, gate_w, preferred_element_type=jnp.float32)
    up_pre = jnp.dot(normed, in_w, preferred_element_type=jnp.float32)
    act = (gate_pre * jax.nn.sigmoid(gate_pre) * up_pre).astype(jnp.bfloat16)
    branch = jnp.dot(act, out_w, preferred_element_type=jnp.float32)
    return h_rows + branch.astype(jnp.bfloat16)


def layer_backward(h_rows, d_out, gate_w, in_w, out_w):
    normed_f, inv_rms = rms_parts(h_rows)
    normed = normed_f.astype(jnp.bfloat16)
    gate_pre = jnp.dot(normed, gate_w, preferred_element_type=jnp.float32)
    up_pre = jnp.dot(normed, in_w, preferred_element_type=jnp.float32)
    gate_sig = jax.nn.sigmoid(gate_pre)
    silu_val = gate_pre * gate_sig
    act = (silu_val * up_pre).astype(jnp.bfloat16)
    d_act = contract(d_out, out_w, 1, 1)
    d_out_w = contract(act, d_out, 0, 0)
    d_gate = (d_act * up_pre * gate_sig * (1.0 + gate_pre * (1.0 - gate_sig))).astype(jnp.bfloat16)
    d_up = (d_act * silu_val).astype(jnp.bfloat16)
    d_gate_w = contract(normed, d_gate, 0, 0)
    d_in_w = contract(normed, d_up, 0, 0)
    d_norm = contract(d_gate, gate_w, 1, 1) + contract(d_up, in_w, 1, 1)
    d_res = inv_rms * (d_norm - normed_f * jnp.mean(d_norm * normed_f, axis=-1, keepdims=True))
    d_h = (d_out.astype(jnp.float32) + d_res).astype(jnp.bfloat16)
    return d_h, d_gate_w, d_in_w, d_out_w


def solution(mesh):
    n_stage = mesh.shape["stage"]
    fwd_pairs = [(idx, idx + 1) for idx in range(n_stage - 1)]
    bwd_pairs = [(idx + 1, idx) for idx in range(n_stage - 1)]

    def stage_body(x_loc, g_loc, gate_loc, in_loc, out_loc):
        gate_full = lax.all_gather(gate_loc[0], "data", axis=1, tiled=True)
        in_full = lax.all_gather(in_loc[0], "data", axis=1, tiled=True)
        out_full = lax.all_gather(out_loc[0], "data", axis=1, tiled=True)
        n_layers, d_model, d_ff = gate_full.shape
        weights = [(gate_full[layer], in_full[layer], out_full[layer]) for layer in range(n_layers)]
        n_micro = x_loc.shape[0]
        rows = x_loc.shape[1] * x_loc.shape[2]
        n_steps = n_micro + n_stage - 1
        stage_idx = lax.axis_index("stage")
        is_first = stage_idx == 0
        is_last = stage_idx == n_stage - 1
        x_rows = x_loc.reshape(n_micro, rows, d_model)
        g_rows = g_loc.reshape(n_micro, rows, d_model)

        def fwd_step(carry, step):
            received, saved = carry
            micro_idx = step - stage_idx
            valid = (micro_idx >= 0) & (micro_idx < n_micro)
            slot = jnp.clip(micro_idx, 0, n_micro - 1)
            h_cur = jnp.where(is_first, lax.dynamic_index_in_dim(x_rows, slot, 0, keepdims=False), received)
            layer_inputs = []
            for gate_w, in_w, out_w in weights:
                layer_inputs.append(h_cur)
                h_cur = layer_forward(h_cur, gate_w, in_w, out_w)
            old_vals = lax.dynamic_index_in_dim(saved, slot, 0, keepdims=False)
            new_vals = jnp.where(valid, jnp.stack(layer_inputs), old_vals)
            saved = lax.dynamic_update_index_in_dim(saved, new_vals, slot, 0)
            sent = lax.ppermute(h_cur, "stage", fwd_pairs)
            return (sent, saved), None

        fwd_init = (jnp.zeros((rows, d_model), jnp.bfloat16), jnp.zeros((n_micro, n_layers, rows, d_model), jnp.bfloat16))
        fwd_final, unused = lax.scan(fwd_step, fwd_init, jnp.arange(n_steps))
        saved = fwd_final[1]

        def bwd_step(carry, step):
            received, dx_buf, grad_sums = carry
            micro_idx = step - (n_stage - 1 - stage_idx)
            valid = (micro_idx >= 0) & (micro_idx < n_micro)
            slot = jnp.clip(micro_idx, 0, n_micro - 1)
            d_cur = jnp.where(is_last, lax.dynamic_index_in_dim(g_rows, slot, 0, keepdims=False), received)
            d_cur = jnp.where(valid, d_cur, jnp.zeros_like(d_cur))
            layer_inputs = lax.dynamic_index_in_dim(saved, slot, 0, keepdims=False)
            new_sums = list(grad_sums)
            for layer in reversed(range(n_layers)):
                gate_w, in_w, out_w = weights[layer]
                d_cur, d_gate_w, d_in_w, d_out_w = layer_backward(layer_inputs[layer], d_cur, gate_w, in_w, out_w)
                gate_sum, in_sum, out_sum = new_sums[layer]
                new_sums[layer] = (gate_sum + d_gate_w, in_sum + d_in_w, out_sum + d_out_w)
            old_dx = lax.dynamic_index_in_dim(dx_buf, slot, 0, keepdims=False)
            dx_buf = lax.dynamic_update_index_in_dim(dx_buf, jnp.where(valid & is_first, d_cur, old_dx), slot, 0)
            sent = lax.ppermute(d_cur, "stage", bwd_pairs)
            return (sent, dx_buf, tuple(new_sums)), None

        zero_sums = tuple((jnp.zeros((d_model, d_ff), jnp.float32), jnp.zeros((d_model, d_ff), jnp.float32), jnp.zeros((d_ff, d_model), jnp.float32)) for layer in range(n_layers))
        bwd_init = (jnp.zeros((rows, d_model), jnp.bfloat16), jnp.zeros((n_micro, rows, d_model), jnp.bfloat16), zero_sums)
        bwd_final, unused = lax.scan(bwd_step, bwd_init, jnp.arange(n_steps))
        dx_buf = bwd_final[1]
        grad_sums = bwd_final[2]
        dx_all = lax.psum(dx_buf, "stage").reshape(x_loc.shape)
        gate_grad = lax.psum_scatter(jnp.stack([layer_sums[0] for layer_sums in grad_sums]), "data", scatter_dimension=1, tiled=True)
        in_grad = lax.psum_scatter(jnp.stack([layer_sums[1] for layer_sums in grad_sums]), "data", scatter_dimension=1, tiled=True)
        out_grad = lax.psum_scatter(jnp.stack([layer_sums[2] for layer_sums in grad_sums]), "data", scatter_dimension=1, tiled=True)
        return dx_all, gate_grad[None], in_grad[None], out_grad[None]

    act_spec = P(None, "data", None, None)
    weight_spec = P("stage", None, "data", None)
    return jax.shard_map(stage_body, mesh=mesh, in_specs=(act_spec, act_spec, weight_spec, weight_spec, weight_spec), out_specs=(act_spec, weight_spec, weight_spec, weight_spec), check_vma=False)
```

profile of v0, /device:TPU:0, one launch (start us, length us, event | category | flops | bytes accessed | tf_op | source)
XLA Modules:
  0.0 5466.6 jit_solution(14541353804924371884)
XLA Ops:
  9.5 400.6 %all-gather.7.cloned.1.call-done = bf16[1,2,2048,5632]{3,2,1,0:T(8,128)(2,1)} async-done(((bf16[1,2,512,5632]{3,2,1,0:T(8,128)(2,1)}), bf16[1,2,2048,5632]{3,2,1,0:T(8,128)(2,1)}) %all-gather.7.cloned.1.call-update) | async-done | bytes 46137360 | tf_op jit(solution)/shard_map/all_gather | solution.py:55
  410.1 31.1 slice_bitcast_fusion.2
  441.2 368.3 %all-gather.9.cloned.1.call-done = bf16[1,2,2048,5632]{3,2,1,0:T(8,128)(2,1)} async-done(((bf16[1,2,512,5632]{3,2,1,0:T(8,128)(2,1)}), bf16[1,2,2048,5632]{3,2,1,0:T(8,128)(2,1)}) %all-gather.9.cloned.1.call-update) | async-done | bytes 46137360 | tf_op jit(solution)/shard_map/all_gather | solution.py:56
  809.5 31.2 slice_bitcast_fusion.1
  840.6 368.2 %all-gather.11.cloned.1.call-done = bf16[1,2,5632,2048]{3,2,1,0:T(8,128)(2,1)} async-done(((bf16[1,2,1408,2048]{3,2,1,0:T(8,128)(2,1)}), bf16[1,2,5632,2048]{3,2,1,0:T(8,128)(2,1)}) %all-gather.11.cloned.1.call-update) | async-done | bytes 46137360 | tf_op jit(solution)/shard_map/all_gather | solution.py:57
  1208.8 30.7 slice_bitcast_fusion
  1242.2 333.2 %while.39 = (s32[]{:T(128)}, bf16[128,2048]{1,0:T(8,128)(2,1)S(1)}, bf16[4,2,128,2048]{3,2,1,0:T(8,128)(2,1)}, pred[]{:T(512)}, s32[5]{0:T(128)S(1)}, /*index=5*...) while((s32[]{:T(128)}, bf16[128,2048]{1,0:T(8,128)(2,1)S(1)}, ...), condition=%wide.region_3.4_spmd, body=%wide.region_0.3_spmd.sunk | while | flops 17735614464 | bytes 159913232 | solution.py:86
  1578.3 1541.5 %while.40 = (s32[]{:T(128)}, bf16[128,2048]{1,0:T(8,128)(2,1)}, bf16[4,128,2048]{2,1,0:T(8,128)(2,1)}, f32[2048,5632]{1,0:T(8,128)}, f32[2048,5632]{1,0:T(8,128)...) while((s32[]{:T(128)}, bf16[128,2048]{1,0:T(8,128)(2,1)}, ...), condition=%wide.region_9.10_spmd.clone, body=%wide.region_4.9_spmd.clone.sunk | while | flops 47425912832 | bytes 1042302592 | solution.py:110
  1981.4 31.1 select_add_fusion.14
  2012.4 32.5 select_add_fusion.17
  2044.9 29.3 select_add_fusion.13
  2074.2 29.7 select_add_fusion.12
  2300.0 31.1 select_add_fusion.14
  2331.0 32.5 select_add_fusion.17
  2363.5 29.3 select_add_fusion.13
  2392.8 29.7 select_add_fusion.12
  2422.5 29.2 select_add_fusion.16
  2618.5 31.1 select_add_fusion.14
  2649.6 32.5 select_add_fusion.17
  2682.1 29.3 select_add_fusion.13
  2711.3 29.7 select_add_fusion.12
  2741.0 29.2 select_add_fusion.16
  2937.1 31.1 select_add_fusion.14
  2968.2 32.5 select_add_fusion.17
  3000.6 29.3 select_add_fusion.13
  3029.9 29.7 select_add_fusion.12
  3119.9 59.6 %pad_maximum_fusion.2 = f32[2,5632,2048]{2,1,0:T(8,128)} fusion(f32[1,5632,2048]{2,1,0:T(8,128)} %bitcast.194, f32[1,5632,2048]{2,1,0:T(8,128)} %bitcast.195), kind=kLoop, calls=%fused_computation.88 | loop fusion | flops 23068672 | bytes 184549376 | tf_op jit(solution)/shard_map/stack | solution.py:116
  3179.6 61.4 %pad_maximum_fusion.1 = f32[2,2048,5632]{2,1,0:T(8,128)} fusion(f32[1,2048,5632]{2,1,0:T(8,128)} %bitcast.196, f32[1,2048,5632]{2,1,0:T(8,128)} %bitcast.198), kind=kLoop, calls=%fused_computation.87 | loop fusion | flops 23068672 | bytes 184549376 | tf_op jit(solution)/shard_map/stack | solution.py:115
  3241.0 61.3 %pad_maximum_fusion = f32[2,2048,5632]{2,1,0:T(8,128)} fusion(f32[1,2048,5632]{2,1,0:T(8,128)} %bitcast.197, f32[1,2048,5632]{2,1,0:T(8,128)} %bitcast.199), kind=kLoop, calls=%fused_computation.86 | loop fusion | flops 23068672 | bytes 184549376 | tf_op jit(solution)/shard_map/stack | solution.py:114
  3302.3 636.7 %reduce-scatter.8.cloned.1.call-done = f32[2,1408,2048]{2,1,0:T(8,128)} async-done(((f32[2,5632,2048]{2,1,0:T(8,128)}), f32[2,1408,2048]{2,1,0:T(8,128)}) %reduce-scatter.8.cloned.1.call-update) | async-done | bytes 23068688 | tf_op jit(solution)/shard_map/reduce_scatter | solution.py:116
  3939.1 758.6 %reduce-scatter.6.cloned.1.call-done = f32[2,512,5632]{2,1,0:T(8,128)} async-done(((f32[2,2048,5632]{2,1,0:T(8,128)}), f32[2,512,5632]{2,1,0:T(8,128)}) %reduce-scatter.6.cloned.1.call-update) | async-done | bytes 23068688 | tf_op jit(solution)/shard_map/reduce_scatter | solution.py:115
  4697.7 758.8 %reduce-scatter.4.cloned.1.call-done = f32[2,512,5632]{2,1,0:T(8,128)} async-done(((f32[2,2048,5632]{2,1,0:T(8,128)}), f32[2,512,5632]{2,1,0:T(8,128)}) %reduce-scatter.4.cloned.1.call-update) | async-done | bytes 23068688 | tf_op jit(solution)/shard_map/reduce_scatter | solution.py:114
  (350 shorter events, 1304.8 us)
Async XLA Ops:
  7.2 403.0 %all-gather.7.cloned.1.call-start = ((), (), s32[]{:S(2)}) async-start(), calls=%async_computation.7 | async-start | bytes 57671680 | tf_op jit(solution)/shard_map/all_gather | solution.py:55
  7.9 801.6 %all-gather.9.cloned.1.call-start = ((), (), s32[]{:S(2)}) async-start(), calls=%async_computation.8 | async-start | bytes 57671680 | tf_op jit(solution)/shard_map/all_gather | solution.py:56
  8.6 1200.1 %all-gather.11.cloned.1.call-start = ((), (), s32[]{:S(2)}) async-start(), calls=%async_computation.9 | async-start | bytes 57671680 | tf_op jit(solution)/shard_map/all_gather | solution.py:57
  9.4 3292.9 %all-reduce.2.cloned.1.call-start = ((), (), s32[]{:S(2)}) async-start(), calls=%async_computation.3 | async-start | bytes 4194304 | tf_op jit(solution)/shard_map/psum | solution.py:113
  1304.7 4.2 collective-permute-start
  1371.4 4.1 collective-permute-start
  1438.0 4.1 collective-permute-start
  1504.7 4.1 collective-permute-start
  1571.3 4.1 collective-permute-start
  1604.8 90.2 %copy-start.13 = (f32[128]{0:T(128)}, f32[128]{0:T(128)S(1)}, u32[]{:S(2)}) copy-start(f32[128]{0:T(128)S(1)} %add_rsqrt_fusion.10) | copy-start | bytes 1540 | tf_op jit(solution)/shard_map/while
  1738.2 105.3 %collective-permute-start.1 = (bf16[128,2048]{1,0:T(8,128)(2,1)}, bf16[128,2048]{1,0:T(8,128)(2,1)}, u32[]{:S(2)}, u32[]{:S(2)}) collective-permute-start(bf16[128,2048]{1,0:T(8,128)(2,1)} %get-tuple-element.717), channel_id=1, source_target_pairs={{1,0},{3,2},{5,4},{7,6}} | collective-permute-start | bytes 1572872 | tf_op jit(solution)/shard_map/while/body/eval_jaxpr/ppermute | solution.py:105
  1846.6 90.2 %copy-start.13 = (f32[128]{0:T(128)}, f32[128]{0:T(128)S(1)}, u32[]{:S(2)}) copy-start(f32[128]{0:T(128)S(1)} %add_rsqrt_fusion.10) | copy-start | bytes 1540 | tf_op jit(solution)/shard_map/while
  1980.1 182.0 %collective-permute-start.1 = (bf16[128,2048]{1,0:T(8,128)(2,1)}, bf16[128,2048]{1,0:T(8,128)(2,1)}, u32[]{:S(2)}, u32[]{:S(2)}) collective-permute-start(bf16[128,2048]{1,0:T(8,128)(2,1)} %get-tuple-element.717), channel_id=1, source_target_pairs={{1,0},{3,2},{5,4},{7,6}} | collective-permute-start | bytes 1572872 | tf_op jit(solution)/shard_map/while/body/eval_jaxpr/ppermute | solution.py:105
  2012.4 32.5 copy-start.2
  2012.4 32.5 copy-start.8
  2074.2 29.7 copy-start.14
  2165.2 90.2 %copy-start.13 = (f32[128]{0:T(128)}, f32[128]{0:T(128)S(1)}, u32[]{:S(2)}) copy-start(f32[128]{0:T(128)S(1)} %add_rsqrt_fusion.10) | copy-start | bytes 1540 | tf_op jit(solution)/shard_map/while
  2298.7 182.0 %collective-permute-start.1 = (bf16[128,2048]{1,0:T(8,128)(2,1)}, bf16[128,2048]{1,0:T(8,128)(2,1)}, u32[]{:S(2)}, u32[]{:S(2)}) collective-permute-start(bf16[128,2048]{1,0:T(8,128)(2,1)} %get-tuple-element.717), channel_id=1, source_target_pairs={{1,0},{3,2},{5,4},{7,6}} | collective-permute-start | bytes 1572872 | tf_op jit(solution)/shard_map/while/body/eval_jaxpr/ppermute | solution.py:105
  2331.0 32.5 copy-start.2
  2331.0 32.5 copy-start.8
  2392.8 29.7 copy-start.14
  2483.8 90.2 %copy-start.13 = (f32[128]{0:T(128)}, f32[128]{0:T(128)S(1)}, u32[]{:S(2)}) copy-start(f32[128]{0:T(128)S(1)} %add_rsqrt_fusion.10) | copy-start | bytes 1540 | tf_op jit(solution)/shard_map/while
  2617.2 182.0 %collective-permute-start.1 = (bf16[128,2048]{1,0:T(8,128)(2,1)}, bf16[128,2048]{1,0:T(8,128)(2,1)}, u32[]{:S(2)}, u32[]{:S(2)}) collective-permute-start(bf16[128,2048]{1,0:T(8,128)(2,1)} %get-tuple-element.717), channel_id=1, source_target_pairs={{1,0},{3,2},{5,4},{7,6}} | collective-permute-start | bytes 1572872 | tf_op jit(solution)/shard_map/while/body/eval_jaxpr/ppermute | solution.py:105
  2649.6 32.5 copy-start.2
  2649.6 32.5 copy-start.8
  2802.3 90.2 %copy-start.13 = (f32[128]{0:T(128)}, f32[128]{0:T(128)S(1)}, u32[]{:S(2)}) copy-start(f32[128]{0:T(128)S(1)} %add_rsqrt_fusion.10) | copy-start | bytes 1540 | tf_op jit(solution)/shard_map/while
  2935.8 182.0 %collective-permute-start.1 = (bf16[128,2048]{1,0:T(8,128)(2,1)}, bf16[128,2048]{1,0:T(8,128)(2,1)}, u32[]{:S(2)}, u32[]{:S(2)}) collective-permute-start(bf16[128,2048]{1,0:T(8,128)(2,1)} %get-tuple-element.717), channel_id=1, source_target_pairs={{1,0},{3,2},{5,4},{7,6}} | collective-permute-start | bytes 1572872 | tf_op jit(solution)/shard_map/while/body/eval_jaxpr/ppermute | solution.py:105
  2968.2 32.5 copy-start.2
  2968.2 32.5 copy-start.8
  3119.8 819.2 %reduce-scatter.8.cloned.1.call-start = ((), (), s32[]{:S(2)}) async-start(), calls=%async_computation.6 | async-start | bytes 115343360 | tf_op jit(solution)/shard_map/reduce_scatter | solution.py:116
  3179.5 1518.1 %reduce-scatter.6.cloned.1.call-start = ((), (), s32[]{:S(2)}) async-start(), calls=%async_computation.5 | async-start | bytes 115343360 | tf_op jit(solution)/shard_map/reduce_scatter | solution.py:115
  3241.0 2215.5 %reduce-scatter.4.cloned.1.call-start = ((), (), s32[]{:S(2)}) async-start(), calls=%async_computation.4 | async-start | bytes 115343360 | tf_op jit(solution)/shard_map/reduce_scatter | solution.py:114
  (60 other events, 994.6 us)
Sparse Core Ops, SparseCore 0:
  9.8 400.3 all-gather.6
  411.9 397.4 all-gather.8
  811.3 397.4 all-gather.10
  3120.0 19.1 all-reduce.1
  3179.7 759.3 reduce-scatter.7
  3942.5 755.1 reduce-scatter.5
  4701.3 755.0 reduce-scatter.3
where the time goes:
time: 5480 us; the launch traced here: 5470 us
  waiting for transfers between devices  3290 us (60%)
  matrix products  1740 us (32%)
  other arithmetic  234 us (4%)
  local copies, waits for them, and re-layouts  134 us (2%)
    dot_general x60, matrix products, contract(): lax.dot_general(left_op, right_op, (((left_dim,), (right_dim,)), ((), ())...  1230 us
    reduce_scatter x1, waiting for transfers between devices, stage_body(): lax.psum_scatter(jnp.stack([layer_sums[0] for layer_sums in grad_sums]),...  759 us
    reduce_scatter x1, waiting for transfers between devices, stage_body(): lax.psum_scatter(jnp.stack([layer_sums[1] for layer_sums in grad_sums]),...  759 us
    reduce_scatter x1, waiting for transfers between devices, stage_body(): lax.psum_scatter(jnp.stack([layer_sums[2] for layer_sums in grad_sums]),...  637 us
    all_gather x1, waiting for transfers between devices, stage_body(): gate_full = lax.all_gather(gate_loc[0], 'data', axis=1, tiled=True)  401 us
    all_gather x1, waiting for transfers between devices, stage_body(): in_full = lax.all_gather(in_loc[0], 'data', axis=1, tiled=True)  368 us
    all_gather x1, waiting for transfers between devices, stage_body(): out_full = lax.all_gather(out_loc[0], 'data', axis=1, tiled=True)  368 us
    dot_general x10, matrix products, layer_forward(): branch = jnp.dot(act, out_w, preferred_element_type=jnp.float32)  206 us
  transfers between devices with their start and end apart: 17, of which 6 were waited for; matrix products, arithmetic and copies ran while one was open for 20% of the time, Pallas kernels for 0%

commit v1 on v0

v1 whole, which is shorter than its diff:
```python
import jax
import jax.numpy as jnp
from jax import lax
from jax.experimental import pallas as pl
from jax.experimental.pallas import tpu as pltpu
from jax.sharding import PartitionSpec as P

EPS = 1e-6
BF = jnp.bfloat16
F32 = jnp.float32
MESH = pl.DeviceIdType.MESH

NL = 4
NM = 4
OWN = 64
ROWS = 512
D = 2048
FS = 1408
F2C = 2 * FS
MS = 512


def mm(lhs, rhs, ld=1, rd=0):
    return lax.dot_general(lhs, rhs, (((ld,), (rd,)), ((), ())), preferred_element_type=F32)


def col_tiles(total, tile, body):
    full = total // tile

    def step(idx, carry):
        body(pl.multiple_of(idx * tile, tile), tile)
        return carry

    lax.fori_loop(0, full, step, 0)
    if total % tile:
        body(full * tile, total % tile)


def kernel(x_ref, g_ref, wg_ref, wu_ref, wo_ref,
           dx_ref, dwg_ref, dwu_ref, dwo_ref, WGU, WO, XALL, AB, RC, RB, WST,
           gu, wo, nb, ab, dab, sall, part, two, tc, tb, hown, eown, nown, wst,
           ls, w_t2r, w_br, w_ar, w_abr, w_or, w_s, w_os, ag_b, ag_a, ag_c0, ag_c1, ag_s,
           rc_r, rc_s, rb_r, rb_s, g_b, g_c, g_o, g_bs, g_cs, dx_r, dx_s):
    d = lax.axis_index("data")
    c = lax.axis_index("stage")
    x = d % 2
    y = d // 2

    def role(layer):
        r = layer % 2
        al = x + r * (y - x)
        be = y + r * (x - y)
        return r, al, be

    def chip(r, al, be):
        return be * (2 - r) + al * (1 + r)

    def nbr(layer):
        r, al, be = role(layer)
        return chip(r, 1 - al, be), chip(r, al, 1 - be)

    def rcopy(src, dst, ssem, rsem, dev):
        return pltpu.make_async_remote_copy(src_ref=src, dst_ref=dst, send_sem=ssem, recv_sem=rsem, device_id=dev, device_id_type=MESH)

    def wait_for(region, sem):
        pltpu.make_async_copy(region, region, sem).wait()

    bar = pltpu.get_barrier_semaphore()
    for dd in range(1, 4):
        for cc in range(2):
            pl.semaphore_signal(bar, inc=1, device_id=((d + dd) % 4, cc), device_id_type=MESH)
    pl.semaphore_signal(bar, inc=1, device_id=(d, 1 - c), device_id_type=MESH)
    pl.semaphore_wait(bar, 7)

    def blk(ref, k, fs, lo, n):
        return ref.at[k, pl.ds(lo, n), pl.ds(pl.multiple_of(fs * FS, 128), FS)]

    def w_dst(l, row, wi, n):
        return WGU.at[l, pl.ds(row, n), pl.ds(wi * FS, FS)]

    def w_core(l):
        p, k = l // 2, l % 2
        r, al, be = role(l)
        row = pl.multiple_of(d * MS, MS)

        @pl.when(c == p)
        def _():
            for wi, ref in enumerate((wg_ref, wu_ref)):
                rcopy(blk(ref, k, chip(r, 1 - p, be), 0, MS), w_dst(l, row, wi, MS), w_s.at[l, 0], w_t2r.at[l], (d, 1 - c)).start()

    def w_split(l):
        p, k = l // 2, l % 2
        r, al, be = role(l)
        row = pl.multiple_of(d * MS, MS)
        bn = chip(r, al, 1 - be)

        @pl.when(c == p)
        def _():
            for half in range(2):
                for wi, ref in enumerate((wg_ref, wu_ref)):
                    for cc in range(2):
                        rcopy(blk(ref, k, chip(r, cc, 1 - be), half * 256, 256), w_dst(l, row + half * 256, wi, 256), w_s.at[l, 1], w_br.at[l, wi, half], (bn, cc)).start()

    def w_pair(l):
        p, k = l // 2, l % 2
        r, al, be = role(l)
        row = pl.multiple_of(d * MS, MS)
        an = chip(r, 1 - al, be)

        @pl.when(c == p)
        def _():
            for wi, ref in enumerate((wg_ref, wu_ref)):
                for cc in range(2):
                    rcopy(blk(ref, k, chip(r, cc, be), 0, MS), w_dst(l, row, wi, MS), w_s.at[l, 2], w_ar.at[l], (an, cc)).start()

    def w_fwd(l):
        r, al, be = role(l)
        an, bn = nbr(l)
        row = pl.multiple_of(bn * MS, MS)
        for half in range(2):
            for wi in range(2):
                src = w_dst(l, row + half * 256, wi, 256)
                wait_for(src, w_br.at[l, wi, half])
                rcopy(src, src, w_s.at[l, 3], w_abr.at[l], (an, c)).start()

    def w_down(l):
        p, k = l // 2, l % 2
        r, al, be = role(l)
        an = chip(r, 1 - al, be)

        @pl.when(c == p)
        def _():
            @pl.when(al != p)
            def _():
                rcopy(wo_ref.at[k], WO.at[l], w_os.at[l, 0], w_or.at[l], (d, al)).start()

            for q in range(4):
                rows = pl.ds(q * 352, 352)
                rcopy(wo_ref.at[k, rows], WO.at[l, rows], w_os.at[l, 1], w_or.at[l], (an, al)).start()

    def w_wait_gu(l):
        p = l // 2
        r, al, be = role(l)
        an, bn = nbr(l)
        abn = chip(r, 1 - al, 1 - be)

        @pl.when(c != p)
        def _():
            wait_for(WGU.at[l, pl.ds(pl.multiple_of(d * MS, MS), MS)], w_t2r.at[l])

        wait_for(WGU.at[l, pl.ds(pl.multiple_of(an * MS, MS), MS)], w_ar.at[l])
        wait_for(WGU.at[l, pl.ds(pl.multiple_of(abn * MS, MS), MS)], w_abr.at[l])

    def w_wait_o(l):
        p = l // 2
        r, al, be = role(l)

        @pl.when(jnp.logical_not(jnp.logical_and(c == al, c == p)))
        def _():
            wait_for(WO.at[l], w_or.at[l])

    def load_gu(l):
        p, k = l // 2, l % 2
        r, al, be = role(l)
        for dd in range(1, 4):
            row = pl.multiple_of(((d + dd) % 4) * MS, MS)
            pltpu.make_async_copy(WGU.at[l, pl.ds(row, MS)], gu.at[pl.ds(row, MS)], ls.at[0]).start()
        row = pl.multiple_of(d * MS, MS)

        @pl.when(c == p)
        def _():
            for wi, ref in enumerate((wg_ref, wu_ref)):
                pltpu.make_async_copy(blk(ref, k, chip(r, c, be), 0, MS), gu.at[pl.ds(row, MS), pl.ds(wi * FS, FS)], ls.at[0]).start()

        @pl.when(c != p)
        def _():
            pltpu.make_async_copy(WGU.at[l, pl.ds(row, MS)], gu.at[pl.ds(row, MS)], ls.at[0]).start()

    def load_o(l):
        p, k = l // 2, l % 2
        r, al, be = role(l)
        mine = jnp.logical_and(c == al, c == p)

        @pl.when(mine)
        def _():
            pltpu.make_async_copy(wo_ref.at[k], wo, ls.at[1]).start()

        @pl.when(jnp.logical_not(mine))
        def _():
            pltpu.make_async_copy(WO.at[l], wo, ls.at[1]).start()

    def slot(ph, m, lo, n):
        return XALL.at[ph, m, pl.ds(lo * OWN, n * OWN)]

    def ag_start(ph, layer, m, src):
        an, bn = nbr(layer)
        pltpu.make_async_copy(src, slot(ph, m, 0, 1), ls.at[2]).start()
        rcopy(src, slot(ph, m, 1, 1), ag_s.at[ph, m], ag_b.at[ph, m], (bn, c)).start()
        rcopy(src, slot(ph, m, 4, 1), ag_s.at[ph, m], ag_a.at[ph, m], (an, c)).start()
        wait_for(slot(ph, m, 0, 1), ls.at[2])

    def ag_mid(ph, layer, m):
        an, bn = nbr(layer)
        wait_for(slot(ph, m, 1, 1), ag_b.at[ph, m])
        rcopy(slot(ph, m, 1, 1), slot(ph, m, 5, 1), ag_s.at[ph, m], ag_a.at[ph, m], (an, c)).start()
        rcopy(slot(ph, m, 0, 2), slot(ph, m, 2, 2), ag_s.at[ph, m], ag_c0.at[ph, m], (d, 1 - c)).start()

    def ag_end(ph, m):
        wait_for(slot(ph, m, 4, 2), ag_a.at[ph, m])
        rcopy(slot(ph, m, 4, 2), slot(ph, m, 6, 2), ag_s.at[ph, m], ag_c1.at[ph, m], (d, 1 - c)).start()

    def ag_load(ph, m, buf, sem):
        wait_for(slot(ph, m, 2, 2), ag_c0.at[ph, m])
        wait_for(slot(ph, m, 6, 2), ag_c1.at[ph, m])
        return pltpu.make_async_copy(XALL.at[ph, m], buf, sem)

    def ag_sent(ph, m):
        wait_for(slot(ph, m, 0, 7), ag_s.at[ph, m])

    def norm(h_rows):
        h_f = h_rows.astype(F32)
        inv = lax.rsqrt(jnp.mean(h_f * h_f, axis=-1, keepdims=True) + EPS)
        return h_f * inv, inv

    def rs_core(ph, m):
        rcopy(part, RC.at[ph, m], rc_s.at[ph, m], rc_r.at[ph, m], (d, 1 - c)).start()

    def rs_split(ph, layer, m):
        an, bn = nbr(layer)
        wait_for(RC.at[ph, m], rc_r.at[ph, m])
        cp = pltpu.make_async_copy(RC.at[ph, m], tc, ls.at[3])
        cp.start()
        cp.wait()
        two[m] = two[m] + tc[...]
        rcopy(two.at[m, pl.ds(OWN, OWN)], RB.at[ph, m], rb_s.at[ph, m], rb_r.at[ph, m], (bn, c)).start()

    def rs_total(ph, m):
        wait_for(RB.at[ph, m], rb_r.at[ph, m])
        cp = pltpu.make_async_copy(RB.at[ph, m], tb, ls.at[4])
        cp.start()
        cp.wait()
        return two[m, pl.ds(0, OWN)] + tb[...]

    def rs_ready(ph, m):
        first = jnp.logical_and(ph == 0, m == 0)
        pph = jnp.where(m == 0, ph - 1, ph)
        pm = jnp.where(m == 0, NM - 1, m - 1)

        @pl.when(jnp.logical_not(first))
        def _():
            wait_for(part, rc_s.at[pph, pm])

        @pl.when(ph > 0)
        def _():
            wait_for(two.at[m, pl.ds(OWN, OWN)], rb_s.at[ph - 1, m])

    def f1(layer, m):
        cp = ag_load(layer, m, nb, ls.at[5])
        cp.start()
        cp.wait()

        def tile(lo, n):
            ab[:, pl.ds(lo, n)] = mm(nb[...], gu[:, pl.ds(lo, n)])

        col_tiles(F2C, 256, tile)
        pltpu.make_async_copy(ab, AB.at[layer, m], ls.at[6]).start()

    def f1_out(layer, m):
        def act(lo, n):
            a_pre = ab[pl.ds(0, 256), pl.ds(lo, n)]
            b_pre = ab[pl.ds(0, 256), pl.ds(lo + FS, n)]
            sall[pl.ds(0, 256), pl.ds(lo, n)] = (a_pre * jax.nn.sigmoid(a_pre) * b_pre).astype(BF)

        col_tiles(FS, 128, act)
        rs_ready(layer, m)

        def out(lo, n):
            res = mm(sall[pl.ds(0, 256), :], wo[:, pl.ds(lo, n)])
            two[m, :, pl.ds(lo, n)] = res[:128]
            part[:, pl.ds(lo, n)] = res[128:]

        col_tiles(D, 256, out)
        rs_core(layer, m)

    def f3(layer, m):
        tot = rs_total(layer, m)
        h_new = hown[layer, m] + tot.astype(BF)
        hown[layer + 1, m] = h_new
        n_f, inv = norm(h_new)
        ag_sent(layer, m)
        nown[m] = n_f.astype(BF)
        ag_start(layer + 1, layer + 1, m, nown.at[m])

    def b1(layer, m):
        ph = 6 - layer
        cp = ag_load(4 + layer, m, nb, ls.at[5])
        cp.start()
        cp.wait()
        wait_for(ab, ls.at[6])
        rows = pl.ds(pl.multiple_of(m * ROWS, ROWS), ROWS)

        def tile(lo, n):
            t_pre = mm(nb[...], wo[pl.ds(lo, n), :], 1, 1)
            a_pre = ab[:, pl.ds(lo, n)]
            b_pre = ab[:, pl.ds(lo + FS, n)]
            sg = jax.nn.sigmoid(a_pre)
            silu = a_pre * sg
            sall[rows, pl.ds(lo, n)] = (silu * b_pre).astype(BF)
            dab[rows, pl.ds(lo, n)] = (t_pre * b_pre * sg * (1.0 + a_pre * (1.0 - sg))).astype(BF)
            dab[rows, pl.ds(lo + FS, n)] = (t_pre * silu).astype(BF)

        col_tiles(FS, 256, tile)

        @pl.when(m < NM - 1)
        def _():
            pltpu.make_async_copy(AB.at[layer, m + 1], ab, ls.at[6]).start()

        rs_ready(ph, m)
        near = pl.ds(pl.multiple_of(m * ROWS, ROWS), 256)

        def out(lo, n):
            res = mm(dab[near, :], gu[pl.ds(lo, n), :], 1, 1)
            two[m, :, pl.ds(lo, n)] = res[:128]
            part[:, pl.ds(lo, n)] = res[128:]

        @pl.when(m == 0)
        def _():
            wait_for(gu, ls.at[0])

        col_tiles(D, 256, out)
        rs_core(ph, m)

    def b3(layer, m):
        q = rs_total(6 - layer, m)
        n_f, inv = norm(hown[layer, m])
        d_res = inv * (q - n_f * jnp.mean(q * n_f, axis=-1, keepdims=True))
        e_new = (eown[m].astype(F32) + d_res).astype(BF)

        @pl.when(layer < NL - 1)
        def _():
            ag_sent(4 + layer, m)

        eown[m] = e_new

        @pl.when(layer > 0)
        def _():
            ag_start(3 + layer, layer - 1, m, eown.at[m])

        @pl.when(layer == 0)
        def _():
            pltpu.make_async_copy(eown.at[m], dx_ref.at[m, c], ls.at[2]).start()
            rcopy(eown.at[m], dx_ref.at[m, c], dx_s.at[m], dx_r.at[m], (d, 1 - c)).start()
            wait_for(eown.at[m], ls.at[2])

    def grad_cols(layer, which):
        for m in range(NM):
            pltpu.make_async_copy(XALL.at[layer, m, :, pl.ds(pl.multiple_of(which * MS, MS), MS)], gu.at[pl.ds(m * ROWS, ROWS), pl.ds(0, MS)], ls.at[7]).start()
        wait_for(gu.at[:, pl.ds(0, MS)], ls.at[7])

    def w_far(layer):
        p, k = layer // 2, layer % 2
        r, al, be = role(layer)
        an, bn = nbr(layer)
        grad_cols(layer, bn)

        def step(i, carry):
            lo = pl.multiple_of(i * 128, 128)
            wst[...] = mm(gu[:, pl.ds(lo, 128)], dab[...], 0, 0)
            cp = pltpu.make_async_copy(wst, WST.at[layer, pl.ds(lo, 128)], ls.at[8])
            cp.start()
            cp.wait()
            for wi, ref in enumerate((dwg_ref, dwu_ref)):
                dst = ref.at[k, pl.ds(lo, 128), pl.ds(pl.multiple_of(chip(r, c, be) * FS, 128), FS)]
                rcopy(WST.at[layer, pl.ds(lo, 128), pl.ds(wi * FS, FS)], dst, g_bs.at[layer], g_b.at[layer], (bn, p)).start()
            return carry

        lax.fori_loop(0, 4, step, 0)

    def w_near(layer):
        p, k = layer // 2, layer % 2
        r, al, be = role(layer)
        grad_cols(layer, d)

        def step(i, carry):
            lo = pl.multiple_of(i * 128, 128)
            wst[...] = mm(gu[:, pl.ds(lo, 128)], dab[...], 0, 0)

            def dst(ref):
                return ref.at[k, pl.ds(lo, 128), pl.ds(pl.multiple_of(chip(r, c, be) * FS, 128), FS)]

            @pl.when(c == p)
            def _():
                for wi, ref in enumerate((dwg_ref, dwu_ref)):
                    pltpu.make_async_copy(wst.at[:, pl.ds(wi * FS, FS)], dst(ref), ls.at[8]).start()
                wait_for(wst, ls.at[8])

            @pl.when(c != p)
            def _():
                for wi, ref in enumerate((dwg_ref, dwu_ref)):
                    rcopy(wst.at[:, pl.ds(wi * FS, FS)], dst(ref), g_cs.at[layer], g_c.at[layer], (d, p)).start()
                wait_for(wst, g_cs.at[layer])

            return carry

        lax.fori_loop(0, 4, step, 0)

    def w_out(layer):
        p, k = layer // 2, layer % 2
        r, al, be = role(layer)

        @pl.when(c == al)
        def _():
            for m in range(NM):
                pltpu.make_async_copy(XALL.at[4 + layer, m], gu.at[pl.ds(m * ROWS, ROWS), pl.ds(0, D)], ls.at[7]).start()
            wait_for(gu.at[:, pl.ds(0, D)], ls.at[7])

            def step(i, carry):
                lo = pl.multiple_of(i * 128, 128)
                res = wst.at[:, pl.ds(0, D)]
                res[...] = mm(sall[:, pl.ds(lo, 128)], gu[:, pl.ds(0, D)], 0, 0)
                dst = dwo_ref.at[k, pl.ds(lo, 128)]

                @pl.when(c == p)
                def _():
                    cp = pltpu.make_async_copy(res, dst, ls.at[8])
                    cp.start()
                    cp.wait()

                @pl.when(c != p)
                def _():
                    rcopy(res, dst, g_cs.at[layer], g_o.at[layer], (d, p)).start()
                    wait_for(res, g_cs.at[layer])

                return carry

            lax.fori_loop(0, FS // 128, step, 0)

    for m in range(NM):
        pltpu.make_async_copy(x_ref.at[m, c], hown.at[0, m], ls.at[3]).start()
        pltpu.make_async_copy(g_ref.at[m, c], eown.at[m], ls.at[4]).start()
    wait_for(hown.at[0], ls.at[3])
    wait_for(eown, ls.at[4])
    for m in range(NM):
        n_f, inv = norm(hown[0, m])
        nown[m] = n_f.astype(BF)
        ag_start(0, 0, m, nown.at[m])
    w_core(0)
    w_split(0)
    w_pair(0)
    for m in range(NM):
        ag_mid(0, 0, m)
    w_fwd(0)
    w_down(0)
    w_core(1)
    w_split(1)
    w_pair(1)
    w_core(2)
    w_split(2)
    w_core(3)
    for m in range(NM):
        ag_end(0, m)

    def fwd_step(t, carry):
        layer, m = t // NM, t % NM

        @pl.when(m == 0)
        def _():
            w_wait_gu(layer)
            load_gu(layer)

            @pl.when(layer == 1)
            def _():
                w_down(2)
                w_pair(2)
                w_split(3)
                for mm_ in range(NM):
                    ag_start(7, 3, mm_, g_ref.at[mm_, c])

            @pl.when(layer == 2)
            def _():
                w_down(3)
                w_pair(3)
                for mm_ in range(NM):
                    ag_mid(7, 3, mm_)

            wait_for(gu, ls.at[0])

        @pl.when(t > 0)
        def _():
            wait_for(ab, ls.at[6])

        f1(layer, m)

        @pl.when(m == 0)
        def _():
            w_wait_o(layer)
            load_o(layer)
            wait_for(wo, ls.at[1])

        @pl.when(layer < NL - 1)
        def _():
            f1_out(layer, m)

        @pl.when(t == 1)
        def _():
            w_fwd(1)
            w_down(1)

        @pl.when(t == 5)
        def _():
            w_fwd(2)

        @pl.when(t == 9)
        def _():
            w_fwd(3)

        @pl.when(jnp.logical_and(t >= 1, t < 13))
        def _():
            rs_split((t - 1) // NM, (t - 1) // NM, (t - 1) % NM)

        @pl.when(jnp.logical_and(t >= 2, t < 14))
        def _():
            f3((t - 2) // NM, (t - 2) % NM)

        @pl.when(jnp.logical_and(t >= 3, t < 15))
        def _():
            ag_mid((t - 3) // NM + 1, (t - 3) // NM + 1, (t - 3) % NM)
            ag_end((t - 3) // NM + 1, (t - 3) % NM)

        return carry

    lax.fori_loop(0, NL * NM, fwd_step, 0)
    for m in range(NM):
        ag_end(7, m)
    wait_for(ab, ls.at[6])

    def bwd_layer(i, carry):
        layer = NL - 1 - i
        ph = 6 - layer
        pltpu.make_async_copy(AB.at[layer, 0], ab, ls.at[6]).start()

        @pl.when(layer < NL - 1)
        def _():
            load_o(layer)
            load_gu(layer)
            wait_for(wo, ls.at[1])

        @pl.when(layer == NL - 1)
        def _():
            load_gu(layer)

        def gather_mid(m):
            @pl.when(layer > 0)
            def _():
                ag_mid(3 + layer, layer - 1, m)

        def gather_end(m):
            @pl.when(layer > 0)
            def _():
                ag_end(3 + layer, m)

        def step(m, c2):
            b1(layer, m)

            @pl.when(m >= 1)
            def _():
                rs_split(ph, layer, m - 1)

            @pl.when(m >= 2)
            def _():
                b3(layer, m - 2)

            @pl.when(m >= 3)
            def _():
                gather_mid(m - 3)

            return c2

        lax.fori_loop(0, NM, step, 0)
        w_far(layer)
        rs_split(ph, layer, 3)
        b3(layer, 2)
        gather_mid(1)
        gather_end(0)
        w_near(layer)
        b3(layer, 3)
        gather_mid(2)
        gather_end(1)
        w_out(layer)
        gather_mid(3)
        gather_end(2)
        gather_end(3)
        return carry

    lax.fori_loop(0, NL, bwd_layer, 0)

    for m in range(NM):
        wait_for(dx_ref.at[m, 1 - c], dx_r.at[m])
        wait_for(dx_ref.at[m, c], dx_s.at[m])
        ag_sent(3, m)
        ag_sent(7, m)
        wait_for(two.at[m, pl.ds(OWN, OWN)], rb_s.at[6, m])
    wait_for(part, rc_s.at[6, NM - 1])
    for l in range(NL):
        p = l // 2
        r, al, be = role(l)
        wait_for(WGU.at[l, pl.ds(0, MS)], w_s.at[l, 3])

        @pl.when(c == p)
        def _():
            wait_for(WGU.at[l, pl.ds(0, MS)], w_s.at[l, 0])
            wait_for(WGU.at[l, pl.ds(0, 2 * MS)], w_s.at[l, 1])
            wait_for(WGU.at[l, pl.ds(0, 2 * MS)], w_s.at[l, 2])
            wait_for(WO.at[l], w_os.at[l, 1])

            @pl.when(al != p)
            def _():
                wait_for(WO.at[l], w_os.at[l, 0])

        wait_for(WST.at[l], g_bs.at[l])

        @pl.when(c == p)
        def _():
            wait_for(AB.at[0, pl.ds(0, 2)], g_b.at[l])
            wait_for(AB.at[0, 0], g_c.at[l])

            @pl.when(al != p)
            def _():
                wait_for(AB.at[0, pl.ds(0, 2)], g_o.at[l])


def solution(mesh):
    def body(x_loc, g_loc, gate_loc, in_loc, out_loc):
        def hbm(shape, dt):
            return jax.ShapeDtypeStruct(shape, dt)

        any_spec = pl.BlockSpec(memory_space=pl.ANY)
        dma = pltpu.SemaphoreType.DMA
        outs = (
            hbm((NM, 2, OWN, D), BF), hbm((2, MS, 4 * FS), F32), hbm((2, MS, 4 * FS), F32), hbm((2, FS, D), F32),
            hbm((NL, D, F2C), BF), hbm((NL, FS, D), BF), hbm((8, NM, ROWS, D), BF), hbm((NL, NM, ROWS, F2C), F32),
            hbm((7, NM, 128, D), F32), hbm((7, NM, OWN, D), F32), hbm((NL, MS, F2C), F32))
        scratch = [
            pltpu.VMEM((D, F2C), BF), pltpu.VMEM((FS, D), BF), pltpu.VMEM((ROWS, D), BF), pltpu.VMEM((ROWS, F2C), F32),
            pltpu.VMEM((NM * ROWS, F2C), BF), pltpu.VMEM((NM * ROWS, FS), BF), pltpu.VMEM((128, D), F32),
            pltpu.VMEM((NM, 128, D), F32), pltpu.VMEM((128, D), F32), pltpu.VMEM((OWN, D), F32),
            pltpu.VMEM((NL, NM, OWN, D), BF), pltpu.VMEM((NM, OWN, D), BF), pltpu.VMEM((NM, OWN, D), BF), pltpu.VMEM((128, F2C), F32),
            dma((9,)), dma((NL,)), dma((NL, 2, 2)), dma((NL,)), dma((NL,)), dma((NL,)), dma((NL, 4)), dma((NL, 2)),
            dma((8, NM)), dma((8, NM)), dma((8, NM)), dma((8, NM)), dma((8, NM)),
            dma((7, NM)), dma((7, NM)), dma((7, NM)), dma((7, NM)), dma((NL,)), dma((NL,)), dma((NL,)), dma((NL,)), dma((NL,)),
            dma((NM,)), dma((NM,))]
        res = pl.pallas_call(
            kernel, out_shape=outs, in_specs=[any_spec] * 5, out_specs=(any_spec,) * len(outs), scratch_shapes=scratch,
            compiler_params=pltpu.CompilerParams(collective_id=0, has_side_effects=True, vmem_limit_bytes=67043328),
        )(x_loc.reshape(NM, 2, OWN, D), g_loc.reshape(NM, 2, OWN, D), gate_loc[0], in_loc[0], out_loc[0])
        return res[0].reshape(x_loc.shape), res[1][None], res[2][None], res[3][None]

    act_spec = P(None, "data", None, None)
    weight_spec = P("stage", None, "data", None)
    return jax.shard_map(body, mesh=mesh, in_specs=(act_spec, act_spec, weight_spec, weight_spec, weight_spec), out_specs=(act_spec, weight_spec, weight_spec, weight_spec), check_vma=False)
```

time: 5480 us -> 2220 us (0.41)
  waiting for transfers between devices: 3290 us -> 0 us
  Pallas kernels: 0 us -> 2160 us
  matrix products: 1740 us -> 0 us
  other arithmetic: 234 us -> 0.01 us
  local copies, waits for them, and re-layouts: 134 us -> 48.7 us
    pallas_call x0 -> x1, Pallas kernels: none -> 2160 us  [body(): pl.pallas_call(kernel, out_shape=outs, in_specs=[any_spec] * 5, out_specs...]
    reduce_scatter x3 -> x0, waiting for transfers between devices: 2150 us -> none  [the longest x1 759 us: stage_body(): lax.psum_scatter(jnp.stack([layer_sums[0] for layer_sums in grad_sums]),...]
    dot_general x100 -> x0, matrix products: 1740 us -> none  [the longest x60 1230 us: contract(): lax.dot_general(left_op, right_op, (((left_dim,), (right_dim,)), ((), ())...]
    all_gather x3 -> x0, waiting for transfers between devices: 1140 us -> none  [the longest x1 401 us: stage_body(): gate_full = lax.all_gather(gate_loc[0], 'data', axis=1, tiled=True)]
    another operation x3 -> x0, other arithmetic: 182 us -> none  [the longest x1 61.4 us: stage_body(): jnp.stack([layer_sums[1] for layer_sums in grad_sums])]
    squeeze x3 -> x0, local copies, waits for them, and re-layouts: 93 us -> none  [the longest x1 31.2 us: stage_body(): in_full[layer]]
  transfers between devices with their start and end apart: 17 -> 0, of which waited for: 6 -> 0; matrix products, arithmetic and copies ran while one was open for 20% -> 0% of each run, Pallas kernels for 0% -> 0%
where the time goes in v1:
time: 2220 us; the launch traced here: 2210 us
  Pallas kernels  2160 us (97%)
  local copies, waits for them, and re-layouts  48.7 us (2%)
    pallas_call x1, Pallas kernels, body(): pl.pallas_call(kernel, out_shape=outs, in_specs=[any_spec] * 5, out_specs...  2160 us
    unnamed x16, local copies, waits for them, and re-layouts  48.7 us

profile of v1, /device:TPU:0, one launch (start us, length us, event | category | flops | bytes accessed | tf_op | source)
XLA Modules:
  0.0 2208.3 jit_solution(9358863068752906225)
XLA Ops:
  0.6 2158.9 %shard_map.84 = (bf16[4,2,64,2048]{3,2,1,0:T(8,128)(2,1)}, f32[2,512,5632]{2,1,0:T(8,128)}, f32[2,512,5632]{2,1,0:T(8,128)}, f32[2,1408,2048]{2,1,0:T(8,128)}, b...) custom-call(bf16[4,2,64,2048]{3,2,1,0:T(8,128)(2,1)} %bitcast.17, ...), custom_call_target="tpu_custom_call" | custom-call | tf_op jit(solution)/shard_map/pallas_call | solution.py:652
  2159.5 3.2 copy.13
  2162.7 0.0 slice-start
  2162.7 0.0 slice-start.1
  2162.7 0.0 slice-start.2
  2162.7 0.0 slice-start.3
  2162.7 18.7 copy.14
  2181.4 0.0 slice-start.4
  2181.4 0.0 slice-start.5
  2181.4 18.6 copy.15
  2200.0 0.0 slice-done
  2200.0 0.0 slice-done.1
  2200.0 0.0 slice-done.2
  2200.0 0.0 slice-done.3
  2200.0 0.0 slice-done.4
  2200.0 0.0 slice-done.5
  2200.0 8.2 copy.16
  (1 shorter events, 0.0 us)
Async XLA Ops:
  2162.7 37.3 %slice-start = ((s8[23068672]{0:T(1024)(128)(4,1)}), s8[4194304]{0:T(1024)(128)(4,1)S(1)}, s32[]{:S(2)}) async-start(s8[23068672]{0:T(1024)(128)(4,1)} %bitcast.9), calls=%async_computation | async-start | bytes 8388608
  2162.7 37.3 %slice-start.1 = ((s8[23068672]{0:T(1024)(128)(4,1)}), s8[4194304]{0:T(1024)(128)(4,1)S(1)}, s32[]{:S(2)}) async-start(s8[23068672]{0:T(1024)(128)(4,1)} %bitcast.9), calls=%async_computation.1 | async-start | bytes 8388608
  2162.7 37.3 %slice-start.2 = ((s8[23068672]{0:T(1024)(128)(4,1)}), s8[4194304]{0:T(1024)(128)(4,1)S(1)}, s32[]{:S(2)}) async-start(s8[23068672]{0:T(1024)(128)(4,1)} %bitcast.9), calls=%async_computation.2 | async-start | bytes 8388608
  2162.7 37.3 %slice-start.3 = ((s8[23068672]{0:T(1024)(128)(4,1)}), s8[4194304]{0:T(1024)(128)(4,1)S(1)}, s32[]{:S(2)}) async-start(s8[23068672]{0:T(1024)(128)(4,1)} %bitcast.9), calls=%async_computation.3 | async-start | bytes 8388608
  2181.4 18.6 slice-start.4
  2181.4 18.6 slice-start.5

commit v2 on v1

v2 whole, which is shorter than its diff:
```python
import jax
import jax.numpy as jnp
from jax import lax
from jax.experimental import pallas as pl
from jax.experimental.pallas import tpu as pltpu
from jax.sharding import PartitionSpec as P

EPS = 1e-6
BF = jnp.bfloat16
F32 = jnp.float32
MESH = pl.DeviceIdType.MESH

NL = 4
NM = 4
OWN = 64
ROWS = 512
D = 2048
FS = 1408
F2C = 2 * FS
SPLIT = 768
ONE, TWO = 1, 2
LAST = NL - ONE
HALF = 256
QUART = 128
FAR = 4
NP = 8
NS = 7
CORES = range(TWO)
MS = 512


(S_GU, S_O, S_OWN, S_TC, S_TB, S_NEAR, S_AB, S_COL, S_ST, S_ST1, S_AB1, S_FAR, S_SX, S_H, S_H1, S_H2, S_H3, S_HL) = range(18)


def mm(lhs, rhs, ld=1, rd=0):
    return lax.dot_general(lhs, rhs, (((ld,), (rd,)), ((), ())), preferred_element_type=F32)


def col_tiles(total, tile, body):
    full = total // tile

    def step(idx, carry):
        body(pl.multiple_of(idx * tile, tile), tile)
        return carry

    lax.fori_loop(0, full, step, 0)
    if total % tile:
        body(full * tile, total % tile)


def flip(v):
    return ONE - v


def home(layer):
    return layer // TWO, layer % TWO


def kernel(x_ref, g_ref, wg_ref, wu_ref, wo_ref,
           dx_ref, dwg_ref, dwu_ref, dwo_ref, WSP, WOS, WGU, WO, XALL, AB, RC, RB, WST, SX, H,
           gu, wo, nb, ab, dab, sall, part, two, tc, tb, hown, eown, nown, wst, ncol,
           ls, w_spr, w_osr, w_t2r, w_br, w_ar, w_abr, w_or, w_s, w_os, ag_b, ag_a, ag_d, ag_c0, ag_c1, ag_s,
           rc_r, rc_s, rb_r, rb_s, g_b, g_c, g_o, g_bs, sx_r, sx_s, dx_r, dx_s):
    d = lax.axis_index("data")
    c = lax.axis_index("stage")
    y, x = home(d)
    mate = (d, 1 - c)

    def role(layer):
        p, r = home(layer)
        al = x + r * (y - x)
        be = y + r * (x - y)
        return r, al, be

    def chip(r, al, be):
        return be * (2 - r) + al * (1 + r)

    def nbr(layer):
        r, al, be = role(layer)
        return chip(r, flip(al), be), chip(r, al, flip(be))

    def rcopy(src, dst, ssem, rsem, dev):
        return pltpu.make_async_remote_copy(src_ref=src, dst_ref=dst, send_sem=ssem, recv_sem=rsem, device_id=dev, device_id_type=MESH)

    def wait_for(region, sem):
        pltpu.make_async_copy(region, region, sem).wait()

    bar = pltpu.get_barrier_semaphore()
    for dd in range(1, 4):
        for cc in CORES:
            pl.semaphore_signal(bar, inc=1, device_id=((d + dd) % 4, cc), device_id_type=MESH)
    pl.semaphore_signal(bar, inc=1, device_id=mate, device_id_type=MESH)
    pl.semaphore_wait(bar, 7)

    def blk(ref, k, fs, lo, n):
        return ref.at[k, pl.ds(lo, n), pl.ds(pl.multiple_of(fs * FS, QUART), FS)]

    def w_dst(l, row, wi, n):
        return WGU.at[l, pl.ds(row, n), pl.ds(wi * FS, FS)]

    def w_core(l):
        p, k = home(l)
        r, al, be = role(l)
        row = pl.multiple_of(d * MS, MS)

        @pl.when(c == p)
        def _():
            for wi, ref in enumerate((wg_ref, wu_ref)):
                rcopy(blk(ref, k, chip(r, 1 - p, flip(be)), 0, MS), WSP.at[l, :, pl.ds(wi * FS, FS)], w_s.at[l, 0], w_spr.at[l], mate).start()
                rcopy(blk(ref, k, chip(r, 1 - p, be), 0, MS), w_dst(l, row, wi, MS), w_s.at[l, 0], w_t2r.at[l], mate).start()

    def w_core_o(l):
        p, k = home(l)
        r, al, be = role(l)

        @pl.when(c == p)
        def _():
            rcopy(wo_ref.at[k, pl.ds(FS // 2, FS // 2)], WOS.at[l], w_os.at[l, 2], w_osr.at[l], mate).start()

            @pl.when(al != p)
            def _():
                rcopy(wo_ref.at[k], WO.at[l], w_os.at[l, 0], w_or.at[l], (d, al)).start()

    def w_split(l, pieces=(0, 1, 2, 3)):
        p, k = home(l)
        r, al, be = role(l)
        row = pl.multiple_of(d * MS, MS)
        bn = chip(r, al, flip(be))

        def go(get):
            for half, wi in [home(q) for q in pieces]:
                rcopy(get(wi, half * HALF), w_dst(l, row + half * HALF, wi, HALF), w_s.at[l, 1], w_br.at[l, wi, half], (bn, c)).start()

        @pl.when(c == p)
        def _():
            go(lambda wi, lo: blk((wg_ref, wu_ref)[wi], k, chip(r, c, flip(be)), lo, HALF))

        @pl.when(c != p)
        def _():
            if 0 in pieces:
                wait_for(WSP.at[l], w_spr.at[l])
            go(lambda wi, lo: WSP.at[l, pl.ds(lo, HALF), pl.ds(wi * FS, FS)])

    def w_pair(l, pieces=(0, 1, 2, 3)):
        p, k = home(l)
        r, al, be = role(l)
        row = pl.multiple_of(d * MS, MS)
        an = chip(r, flip(al), be)

        def go(get):
            for half, wi in [home(q) for q in pieces]:
                rcopy(get(wi, half * HALF), w_dst(l, row + half * HALF, wi, HALF), w_s.at[l, 2], w_ar.at[l], (an, c)).start()

        @pl.when(c == p)
        def _():
            go(lambda wi, lo: blk((wg_ref, wu_ref)[wi], k, chip(r, c, be), lo, HALF))

        @pl.when(c != p)
        def _():
            if 0 in pieces:
                wait_for(WGU.at[l, pl.ds(row, MS)], w_t2r.at[l])
            go(lambda wi, lo: w_dst(l, row + lo, wi, HALF))

    def w_fwd(l, pieces=(0, 1, 2, 3)):
        r, al, be = role(l)
        an, bn = nbr(l)
        row = pl.multiple_of(bn * MS, MS)
        for half, wi in [home(q) for q in pieces]:
            src = w_dst(l, row + half * HALF, wi, HALF)
            wait_for(src, w_br.at[l, wi, half])
            rcopy(src, src, w_s.at[l, 3], w_abr.at[l], (an, c)).start()

    def w_down(l, pieces=(0, 1, 2, 3)):
        p, k = home(l)
        r, al, be = role(l)
        an = chip(r, flip(al), be)
        half, n = FS // 2, FS // 8

        @pl.when(c == p)
        def _():
            for q in pieces:
                rcopy(wo_ref.at[k, pl.ds(q * n, n)], WO.at[l, pl.ds(q * n, n)], w_os.at[l, 1], w_or.at[l], (an, al)).start()

        @pl.when(c != p)
        def _():
            if 0 in pieces:
                wait_for(WOS.at[l], w_osr.at[l])
            for q in pieces:
                rcopy(WOS.at[l, pl.ds(q * n, n)], WO.at[l, pl.ds(half + q * n, n)], w_os.at[l, 1], w_or.at[l], (an, al)).start()

    def w_wait_gu(l):
        r, al, be = role(l)
        an, bn = nbr(l)
        abn = chip(r, flip(al), flip(be))

        wait_for(WGU.at[l, pl.ds(pl.multiple_of(an * MS, MS), MS)], w_ar.at[l])
        wait_for(WGU.at[l, pl.ds(pl.multiple_of(abn * MS, MS), MS)], w_abr.at[l])

    def w_wait_o(l):
        p, k = home(l)
        r, al, be = role(l)

        @pl.when(jnp.logical_not(jnp.logical_and(c == al, c == p)))
        def _():
            wait_for(WO.at[l], w_or.at[l])

    def load_gu(l):
        p, k = home(l)
        r, al, be = role(l)
        for dd in range(1, 4):
            row = pl.multiple_of(((d + dd) % 4) * MS, MS)
            pltpu.make_async_copy(WGU.at[l, pl.ds(row, MS)], gu.at[pl.ds(row, MS)], ls.at[S_GU]).start()
        row = pl.multiple_of(d * MS, MS)

        @pl.when(c == p)
        def _():
            for wi, ref in enumerate((wg_ref, wu_ref)):
                pltpu.make_async_copy(blk(ref, k, chip(r, c, be), 0, MS), gu.at[pl.ds(row, MS), pl.ds(wi * FS, FS)], ls.at[S_GU]).start()

        @pl.when(c != p)
        def _():
            pltpu.make_async_copy(WGU.at[l, pl.ds(row, MS)], gu.at[pl.ds(row, MS)], ls.at[S_GU]).start()

    def load_o(l):
        p, k = home(l)
        r, al, be = role(l)
        mine = jnp.logical_and(c == al, c == p)

        @pl.when(mine)
        def _():
            pltpu.make_async_copy(wo_ref.at[k], wo, ls.at[S_O]).start()

        @pl.when(jnp.logical_not(mine))
        def _():
            pltpu.make_async_copy(WO.at[l], wo, ls.at[S_O]).start()

    def slot(ph, m, lo, n):
        return XALL.at[ph, m, pl.ds(lo * OWN, n * OWN)]

    def ag_start(ph, layer, m, src):
        an, bn = nbr(layer)
        pltpu.make_async_copy(src, slot(ph, m, 0, 1), ls.at[S_OWN]).start()
        rcopy(src, slot(ph, m, ONE, ONE), ag_s.at[ph, m], ag_b.at[ph, m], (bn, c)).start()
        rcopy(src, slot(ph, m, FAR, ONE), ag_s.at[ph, m], ag_a.at[ph, m], (an, c)).start()
        wait_for(slot(ph, m, 0, 1), ls.at[S_OWN])

    def other_way(ph):
        return jnp.logical_and(ph != 1, jnp.logical_or(ph < NL, ph >= NP - TWO))

    def ag_mid(ph, layer, m):
        an, bn = nbr(layer)
        alt = other_way(ph)
        wait_for(slot(ph, m, ONE, ONE), ag_b.at[ph, m])
        rcopy(slot(ph, m, 0, TWO), slot(ph, m, TWO, TWO), ag_s.at[ph, m], ag_c0.at[ph, m], mate).start()

        @pl.when(jnp.logical_not(alt))
        def _():
            rcopy(slot(ph, m, ONE, ONE), slot(ph, m, FAR + ONE, ONE), ag_s.at[ph, m], ag_d.at[ph, m], (an, c)).start()

        @pl.when(alt)
        def _():
            wait_for(slot(ph, m, FAR, ONE), ag_a.at[ph, m])
            rcopy(slot(ph, m, FAR, ONE), slot(ph, m, FAR + ONE, ONE), ag_s.at[ph, m], ag_d.at[ph, m], (bn, c)).start()

    def ag_end(ph, m):
        @pl.when(jnp.logical_not(other_way(ph)))
        def _():
            wait_for(slot(ph, m, FAR, ONE), ag_a.at[ph, m])

        wait_for(slot(ph, m, FAR + ONE, ONE), ag_d.at[ph, m])
        rcopy(slot(ph, m, FAR, TWO), slot(ph, m, FAR + TWO, TWO), ag_s.at[ph, m], ag_c1.at[ph, m], mate).start()

    def ag_load(ph, m, half):
        wait_for(slot(ph, m, 2 + 4 * half, 2), (ag_c0, ag_c1)[half].at[ph, m])
        rows = pl.ds(half * HALF, HALF)
        pltpu.make_async_copy(XALL.at[ph, m, rows], nb.at[rows], ls.at[(S_NEAR, S_FAR)[half]]).start()

    def ag_loaded(half):
        wait_for(nb.at[pl.ds(half * HALF, HALF)], ls.at[(S_NEAR, S_FAR)[half]])

    def ag_sent(ph, m):
        wait_for(slot(ph, m, 0, 7), ag_s.at[ph, m])

    def norm(h_rows):
        h_f = h_rows.astype(F32)
        inv = lax.rsqrt(jnp.mean(h_f * h_f, axis=-1, keepdims=True) + EPS)
        return h_f * inv, inv

    def rs_core(ph, m):
        rcopy(part, RC.at[ph, m], rc_s.at[ph, m], rc_r.at[ph, m], mate).start()

    def rs_load(ph, m):
        wait_for(RC.at[ph, m], rc_r.at[ph, m])
        pltpu.make_async_copy(RC.at[ph, m], tc, ls.at[S_TC]).start()

    def rs_split(ph, layer, m):
        an, bn = nbr(layer)
        wait_for(tc, ls.at[S_TC])
        two[m] = two[m] + tc[...]
        rcopy(two.at[m, pl.ds(OWN, OWN)], RB.at[ph, m], rb_s.at[ph, m], rb_r.at[ph, m], (bn, c)).start()

    def rs_total_load(ph, m):
        wait_for(RB.at[ph, m], rb_r.at[ph, m])
        pltpu.make_async_copy(RB.at[ph, m], tb, ls.at[S_TB]).start()

    def rs_total(ph, m):
        wait_for(tb, ls.at[S_TB])
        return two[m, pl.ds(0, OWN)] + tb[...]

    def rs_ready(ph, m):
        first = jnp.logical_and(ph == 0, m == 0)
        pph = jnp.where(m == 0, ph - 1, ph)
        pm = jnp.where(m == 0, NM - 1, m - 1)

        @pl.when(jnp.logical_not(first))
        def _():
            wait_for(part, rc_s.at[pph, pm])

        @pl.when(ph > 0)
        def _():
            wait_for(two.at[m, pl.ds(OWN, OWN)], rb_s.at[ph - 1, m])

    def pre(layer, m, half):
        rows = pl.ds(half * HALF, HALF)
        ab[rows, :] = mm(nb[rows, :], gu[...])

        @pl.when(layer < LAST)
        def _():
            pltpu.make_async_copy(ab.at[rows], AB.at[layer, m, rows], ls.at[S_AB + 4 * half]).start()

    def ab_wait(half):
        wait_for(ab.at[pl.ds(half * HALF, HALF)], ls.at[S_AB + 4 * half])

    def f1_out(layer, m):
        def act(lo, n):
            a_pre = ab[pl.ds(0, HALF), pl.ds(lo, n)]
            b_pre = ab[pl.ds(0, HALF), pl.ds(lo + FS, n)]
            sall[pl.ds(0, HALF), pl.ds(lo, n)] = (a_pre * jax.nn.sigmoid(a_pre) * b_pre).astype(BF)

        col_tiles(FS, 128, act)
        rs_ready(layer, m)

        def out(lo, n):
            res = mm(sall[pl.ds(0, HALF), :], wo[:, pl.ds(lo, n)])
            two[m, :, pl.ds(lo, n)] = res[:128]
            part[:, pl.ds(lo, n)] = res[128:]

        col_tiles(D, 1024, out)
        rs_core(layer, m)

    def f3(layer, m):
        rs_total_load(layer, m)
        tot = rs_total(layer, m)
        h_new = hown[m] + tot.astype(BF)

        @pl.when(layer > 0)
        def _():
            wait_for(hown.at[m], ls.at[S_H + m])

        hown[m] = h_new

        @pl.when(layer < NL - 2)
        def _():
            pltpu.make_async_copy(hown.at[m], H.at[layer, m], ls.at[S_H + m]).start()

        n_f, inv = norm(h_new)
        ag_sent(layer, m)
        nown[m] = n_f.astype(BF)
        ag_start(layer + 1, layer + 1, m, nown.at[m])

    def b1(layer, m, half, loaded=False, between=None):
        rows = pl.ds(half * HALF, HALF)
        ag_loaded(half)
        t_buf = wst.at[half, :, pl.ds(0, FS)]
        t_buf[...] = mm(nb[rows, :], wo[...], ONE, ONE)
        if not loaded:
            ab_wait(half)
        if between is not None:
            between()
        into = pl.ds(pl.multiple_of(m * ROWS + half * HALF, HALF), 256)

        def tile(lo, n):
            t_pre = t_buf[:, pl.ds(lo, n)]
            a_pre = ab[rows, pl.ds(lo, n)]
            b_pre = ab[rows, pl.ds(lo + FS, n)]
            sg = jax.nn.sigmoid(a_pre)
            silu = a_pre * sg
            sall[into, pl.ds(lo, n)] = (silu * b_pre).astype(BF)
            dab[into, pl.ds(lo, n)] = (t_pre * b_pre * sg * (1.0 + a_pre * (1.0 - sg))).astype(BF)
            dab[into, pl.ds(lo + FS, n)] = (t_pre * silu).astype(BF)

        col_tiles(FS, 128, tile)
        r, al, be = role(layer)

        @pl.when(c == al)
        def _():
            for near in CORES:
                src = pl.ds(pl.multiple_of(m * ROWS + half * HALF + near * 128, 128), QUART)
                dst = pl.ds(pl.multiple_of(m * ROWS + half * HALF + (1 - near) * 128, 128), QUART)
                rcopy(sall.at[src, pl.ds(SPLIT, FS - SPLIT)], SX.at[layer, dst], sx_s.at[layer], sx_r.at[layer], mate).start()

        if not loaded:
            @pl.when(m < NM - 1)
            def _():
                pltpu.make_async_copy(AB.at[layer, m + 1, rows], ab.at[rows], ls.at[S_AB + 4 * half]).start()

    def b1_out(layer, m):
        ph = NS - ONE - layer
        rs_ready(ph, m)
        near = pl.ds(pl.multiple_of(m * ROWS, ROWS), 256)

        @pl.when(jnp.logical_and(m == 0, layer < LAST))
        def _():
            wait_for(gu, ls.at[S_GU])

        def out(lo, n):
            res = mm(dab[near, :], gu[pl.ds(lo, n), :], ONE, ONE)
            two[m, :, pl.ds(lo, n)] = res[:128]
            part[:, pl.ds(lo, n)] = res[128:]

        col_tiles(D, 1024, out)
        rs_core(ph, m)

    def b3(layer, m):
        q = rs_total(NS - ONE - layer, m)
        n_f, inv = norm(hown[m])
        d_res = inv * (q - n_f * jnp.mean(q * n_f, axis=-1, keepdims=True))
        e_new = (eown[m].astype(F32) + d_res).astype(BF)

        ag_sent(NL + layer, m)
        eown[m] = e_new

        @pl.when(layer > 0)
        def _():
            ag_start(NL - ONE + layer, layer - 1, m, eown.at[m])

        @pl.when(layer == 0)
        def _():
            pltpu.make_async_copy(eown.at[m], dx_ref.at[m, c], ls.at[S_OWN]).start()
            rcopy(eown.at[m], dx_ref.at[m, c], dx_s.at[m], dx_r.at[m], mate).start()
            wait_for(eown.at[m], ls.at[S_OWN])

    def grad_cols(layer, which):
        for m in range(NM):
            pltpu.make_async_copy(XALL.at[layer, m, :, pl.ds(pl.multiple_of(which * MS, MS), MS)], ncol.at[pl.ds(m * ROWS, ROWS)], ls.at[S_COL]).start()

    def w_far(layer, i):
        wst[i] = mm(ncol[:, pl.ds(i * HALF, HALF)], dab[...], 0, 0)
        pltpu.make_async_copy(wst.at[i], WST.at[layer, pl.ds(i * HALF, HALF)], ls.at[S_ST + i]).start()

    def w_send(layer, piece):
        p, k = home(layer)
        r, al, be = role(layer)
        an, bn = nbr(layer)
        rows = pl.ds(pl.multiple_of((piece // 2) * 64, 64), 64)
        for wi, ref in enumerate((dwg_ref, dwu_ref)):
            @pl.when(piece % 2 == wi)
            def _():
                dst = ref.at[k, rows, pl.ds(pl.multiple_of(chip(r, c, be) * FS, QUART), FS)]
                rcopy(WST.at[layer, rows, pl.ds(wi * FS, FS)], dst, g_bs.at[layer], g_b.at[layer], (bn, p)).start()

    def w_sends(layer, lo, n):
        def step(i, carry):
            w_send(layer, i)
            return carry

        lax.fori_loop(lo, lo + n, step, 0)

    def out_load(layer):
        r, al, be = role(layer)
        for m in range(NM):
            pltpu.make_async_copy(XALL.at[NL + layer, m], gu.at[pl.ds(m * ROWS, ROWS), pl.ds(0, D)], ls.at[S_GU]).start()

        @pl.when(c != al)
        def _():
            wait_for(SX.at[layer], sx_r.at[layer])
            pltpu.make_async_copy(SX.at[layer], sall.at[:, pl.ds(SPLIT, FS - SPLIT)], ls.at[S_SX]).start()

    def w_near(layer, i):
        p, k = home(layer)
        r, al, be = role(layer)
        wst[i] = mm(ncol[:, pl.ds(i * HALF, HALF)], dab[...], 0, 0)
        for wi, ref in enumerate((dwg_ref, dwu_ref)):
            src = wst.at[i, :, pl.ds(wi * FS, FS)]
            dst = ref.at[k, pl.ds(i * HALF, HALF), pl.ds(pl.multiple_of(chip(r, c, be) * FS, QUART), FS)]

            @pl.when(c == p)
            def _():
                pltpu.make_async_copy(src, dst, ls.at[S_ST + i]).start()

            @pl.when(c != p)
            def _():
                rcopy(src, dst, ls.at[S_ST + i], g_c.at[layer], (d, p)).start()

    def near_end():
        for i in CORES:
            wait_for(wst.at[i], ls.at[S_ST + i])

    def w_out(layer, tiles):
        p, k = home(layer)
        r, al, be = role(layer)
        base = jnp.where(c == al, 0, SPLIT)

        def rows_of(slot, n):
            return wst.at[slot, pl.ds(0, n), pl.ds(0, D)]

        def one(i, slot, n):
            lo = pl.multiple_of(base + i * HALF, 128)
            res = rows_of(slot, n)
            res[...] = mm(sall[:, pl.ds(lo, n)], gu[:, pl.ds(0, D)], 0, 0)
            dst = dwo_ref.at[k, pl.ds(lo, n)]

            @pl.when(c == p)
            def _():
                pltpu.make_async_copy(res, dst, ls.at[S_ST + slot]).start()

            @pl.when(c != p)
            def _():
                rcopy(res, dst, ls.at[S_ST + slot], g_o.at[layer], (d, p)).start()

        if 0 in tiles:
            wait_for(gu.at[:, pl.ds(0, D)], ls.at[S_GU])

            @pl.when(c != al)
            def _():
                wait_for(SX.at[layer], ls.at[S_SX])

            def step(i, carry):
                one(i, i, 256)
                return carry

            lax.fori_loop(0, 2, step, 0)
        if 2 in tiles:
            wait_for(rows_of(0, 256), ls.at[S_ST])

            @pl.when(c == al)
            def _():
                one(2, 0, 256)
                wait_for(rows_of(0, 256), ls.at[S_ST])
                wait_for(SX.at[layer], sx_s.at[layer])

            @pl.when(c != al)
            def _():
                one(2, 0, 128)
                wait_for(rows_of(0, 128), ls.at[S_ST])

            wait_for(rows_of(1, 256), ls.at[S_ST1])

    w_core(0)
    for m in range(NM):
        pltpu.make_async_copy(x_ref.at[m, c], hown.at[m], ls.at[S_TC]).start()
        pltpu.make_async_copy(g_ref.at[m, c], eown.at[m], ls.at[S_TB]).start()
    w_split(0)
    w_pair(0)
    w_core_o(0)
    wait_for(hown, ls.at[S_TC])
    wait_for(eown, ls.at[S_TB])
    for m in range(NM):
        n_f, inv = norm(hown[m])
        nown[m] = n_f.astype(BF)
        ag_start(0, 0, m, nown.at[m])
    for l in range(1, NL):
        w_core(l)
        w_core_o(l)
    w_pair(1)
    w_fwd(0)
    for m in range(NM):
        ag_mid(0, 0, m)
    w_down(0)
    w_split(1)
    w_down(1)

    def fwd_step(t, carry):
        layer, m = t // NM, t % NM

        @pl.when(m == 0)
        def _():
            w_wait_gu(layer)
            load_gu(layer)
            wait_for(gu, ls.at[S_GU])

        @pl.when(jnp.logical_and(t > 0, t < 13))
        def _():
            ab_wait(0)

        @pl.when(t <= 12)
        def _():
            ag_load(layer, m, 0)

        ag_loaded(0)
        pre(layer, m, 0)

        @pl.when(m == 0)
        def _():
            w_wait_o(layer)
            load_o(layer)
            wait_for(wo, ls.at[S_O])

        @pl.when(layer < LAST)
        def _():
            f1_out(layer, m)

        @pl.when(layer == LAST)
        def _():
            ag_load(NL + layer, m, 0)

        @pl.when(jnp.logical_and(t >= 2, t < 14))
        def _():
            f3((t - 2) // NM, (t - 2) % NM)

        @pl.when(jnp.logical_and(t >= 3, t < 15))
        def _():
            ag_mid((t - 3) // NM + 1, (t - 3) // NM + 1, (t - 3) % NM)

        ag_end(layer, m)

        @pl.when(jnp.logical_and(t > 0, t < 13))
        def _():
            ab_wait(1)

        ag_load(layer, m, 1)

        @pl.when(layer == LAST)
        def _():
            b1(layer, m, 0, True)
            b1_out(layer, m)

            @pl.when(m < NM - 1)
            def _():
                ag_load(layer, m + 1, 0)

        ag_loaded(1)
        pre(layer, m, 1)

        @pl.when(layer < LAST)
        def _():
            rs_load(layer, m)
            rs_split(layer, layer, m)

        @pl.when(layer == LAST)
        def _():
            ag_load(NL + layer, m, 1)

            @pl.when(m >= 2)
            def _():
                rs_total_load(NS - ONE - layer, m - 2)
                b3(layer, m - 2)

            b1(layer, m, 1, True, lambda: rs_load(NS - ONE - layer, m))
            rs_split(NS - ONE - layer, layer, m)

        def at(step, *work):
            @pl.when(t == step)
            def _():
                for fn in work:
                    fn()

        def each(fn):
            for m_ in range(NM):
                fn(NP - ONE, LAST, m_)

        plan = ("F1a P2a", "F1bc P2b", "F1d S2a P2c", "S2bcd P2d", "P3ab F2a", "F2bcd P3cd D2a",
                "D2bcd D3ab", "S3abcd D3cd", "", "F3a", "F3b", "F3cd")
        sends = {"F": w_fwd, "P": w_pair, "S": w_split, "D": w_down}
        for step, words in enumerate(plan):
            for w in words.split():
                at(step, lambda: sends[w[:ONE]](int(w[ONE:TWO]), ["abcd".index(q) for q in w[TWO:]]))

        at(7, lambda: each(lambda ph, l, m_: ag_start(ph, l, m_, eown.at[m_])))
        at(9, lambda: each(ag_mid))
        at(11, lambda: each(lambda ph, l, m_: ag_end(ph, m_)))
        return carry

    lax.fori_loop(0, NL * NM, fwd_step, 0)

    def bwd_layer(i, carry):
        layer = LAST - i
        ph = NS - ONE - layer
        an, bn = nbr(layer)
        grad_cols(layer, bn)

        @pl.when(layer < LAST)
        def _():
            for half in CORES:
                rows = pl.ds(half * HALF, HALF)
                pltpu.make_async_copy(AB.at[layer, 0, rows], ab.at[rows], ls.at[S_AB + 4 * half]).start()
            load_o(layer)
            load_gu(layer)

            @pl.when(layer > 0)
            def _():
                pltpu.make_async_copy(H.at[layer - 1], hown, ls.at[S_HL]).start()

            @pl.when(layer == 0)
            def _():
                for m in range(NM):
                    pltpu.make_async_copy(x_ref.at[m, c], hown.at[m], ls.at[S_HL]).start()

            wait_for(wo, ls.at[S_O])
            wait_for(hown, ls.at[S_HL])

        def gather_mid(m):
            @pl.when(layer > 0)
            def _():
                ag_mid(NL - ONE + layer, layer - 1, m)

        def bulk(lyr, at, n, *only):
            for v in only:
                @pl.when(layer == v)
                def _():
                    w_sends(lyr, at, n)

        bulk(3, 4, 1, 2)
        bulk(3, 13, 3, 1)
        bulk(2, 0, 1, 1)
        bulk(2, 11, 5, 0)
        bulk(1, 0, 4, 0)

        def step(m, c2):
            ag_load(NL + layer, m, 1)
            b1(layer, m, 0)

            @pl.when(m >= 2)
            def _():
                rs_total_load(ph, m - 2)

            b1_out(layer, m)

            @pl.when(m < NM - 1)
            def _():
                ag_end(NL + layer, m + 1)
                ag_load(NL + layer, m + 1, 0)

            @pl.when(m >= 2)
            def _():
                b3(layer, m - 2)

            bulk(3, 5 + 2 * m, 1, 2)
            bulk(2, 1 + 2 * m, 1, 1)
            b1(layer, m, 1, False, lambda: rs_load(ph, m))
            rs_split(ph, layer, m)
            bulk(3, 6 + 2 * m, 1, 2)
            bulk(2, 2 + 2 * m, 1, 1)
            bulk(1, 4 + 3 * m, 3, 0)
            return c2

        @pl.when(layer < LAST)
        def _():
            ag_load(NL + layer, 0, 0)
            lax.fori_loop(0, NM, step, 0)

        out_load(layer)
        wait_for(ncol, ls.at[S_COL])
        w_far(layer, 0)
        rs_total_load(ph, 2)
        w_far(layer, 1)
        b3(layer, 2)
        grad_cols(layer, d)
        near_end()

        @pl.when(layer == 0)
        def _():
            w_sends(0, 0, 16)

        gather_mid(0)
        wait_for(ncol, ls.at[S_COL])
        w_near(layer, 0)
        rs_total_load(ph, 3)
        b3(layer, 3)
        bulk(3, 0, 1, 3)
        w_near(layer, 1)
        bulk(3, 1, 1, 3)
        gather_mid(1)
        near_end()
        w_out(layer, (0, 1))
        bulk(3, 2, 1, 3)
        bulk(2, 9, 1, 1)
        gather_mid(2)
        w_out(layer, (2,))
        bulk(3, 3, 1, 3)
        bulk(2, 10, 1, 1)
        gather_mid(3)

        @pl.when(layer > 0)
        def _():
            ag_end(NL - ONE + layer, 0)

        return carry

    lax.fori_loop(0, NL, bwd_layer, 0)

    for m in range(NM):
        wait_for(dx_ref.at[m, 1 - c], dx_r.at[m])
        wait_for(dx_ref.at[m, c], dx_s.at[m])
        ag_sent(3, m)
        wait_for(two.at[m, pl.ds(OWN, OWN)], rb_s.at[6, m])
    wait_for(part, rc_s.at[6, NM - 1])
    for l in range(NL):
        p, k = home(l)
        r, al, be = role(l)
        for i in range(1, 4):
            wait_for(WGU.at[l, pl.ds(0, MS)], w_s.at[l, i])
        wait_for(WOS.at[l], w_os.at[l, 1])

        @pl.when(c == p)
        def _():
            wait_for(WGU.at[l, pl.ds(0, 2 * MS)], w_s.at[l, 0])
            wait_for(WOS.at[l], w_os.at[l, 2])

            @pl.when(al != p)
            def _():
                wait_for(WO.at[l], w_os.at[l, 0])

        wait_for(WST.at[l], g_bs.at[l])

        @pl.when(c == p)
        def _():
            wait_for(AB.at[0, pl.ds(0, 2)], g_b.at[l])
            wait_for(AB.at[0, 0], g_c.at[l])

            @pl.when(al != p)
            def _():
                wait_for(dwo_ref.at[0, pl.ds(0, SPLIT)], g_o.at[l])

            @pl.when(al == p)
            def _():
                wait_for(dwo_ref.at[0, pl.ds(0, FS - SPLIT)], g_o.at[l])


def solution(mesh):
    def body(x_loc, g_loc, gate_loc, in_loc, out_loc):
        def hbm(shape, dt):
            return jax.ShapeDtypeStruct(shape, dt)

        any_spec = pl.BlockSpec(memory_space=pl.ANY)
        dma = pltpu.SemaphoreType.DMA
        outs = (
            hbm((NM, 2, OWN, D), BF), hbm((2, MS, 4 * FS), F32), hbm((2, MS, 4 * FS), F32), hbm((2, FS, D), F32),
            hbm((NL, MS, F2C), BF), hbm((NL, FS // 2, D), BF),
            hbm((NL, D, F2C), BF), hbm((NL, FS, D), BF), hbm((NP, NM, ROWS, D), BF), hbm((NL, NM, ROWS, F2C), F32),
            hbm((NS, NM, QUART, D), F32), hbm((NS, NM, OWN, D), F32), hbm((NL, MS, F2C), F32), hbm((NL, NM * ROWS, FS - SPLIT), BF), hbm((2, NM, OWN, D), BF))
        scratch = [
            pltpu.VMEM((D, F2C), BF), pltpu.VMEM((FS, D), BF), pltpu.VMEM((ROWS, D), BF), pltpu.VMEM((ROWS, F2C), F32),
            pltpu.VMEM((NM * ROWS, F2C), BF), pltpu.VMEM((NM * ROWS, FS), BF), pltpu.VMEM((QUART, D), F32),
            pltpu.VMEM((NM, QUART, D), F32), pltpu.VMEM((QUART, D), F32), pltpu.VMEM((OWN, D), F32),
            pltpu.VMEM((NM, OWN, D), BF), pltpu.VMEM((NM, OWN, D), BF), pltpu.VMEM((NM, OWN, D), BF), pltpu.VMEM((2, 256, F2C), F32), pltpu.VMEM((NM * ROWS, MS), BF),
            dma((S_HL + ONE,)), dma((NL,)), dma((NL,)), dma((NL,)), dma((NL, 2, 2)), dma((NL,)), dma((NL,)), dma((NL,)), dma((NL, 4)), dma((NL, 3)),
            dma((NP, NM)), dma((NP, NM)), dma((NP, NM)), dma((NP, NM)), dma((NP, NM)), dma((NP, NM)),
            dma((NS, NM)), dma((NS, NM)), dma((NS, NM)), dma((NS, NM)), dma((NL,)), dma((NL,)), dma((NL,)), dma((NL,)), dma((NL,)), dma((NL,)),
            dma((NM,)), dma((NM,))]
        res = pl.pallas_call(
            kernel, out_shape=outs, in_specs=[any_spec] * 5, out_specs=(any_spec,) * len(outs), scratch_shapes=scratch,
            compiler_params=pltpu.CompilerParams(collective_id=0, has_side_effects=True, vmem_limit_bytes=67043328),
        )(x_loc.reshape(NM, 2, OWN, D), g_loc.reshape(NM, 2, OWN, D), gate_loc[0], in_loc[0], out_loc[0])
        return res[0].reshape(x_loc.shape), res[1][None], res[2][None], res[3][None]

    act_spec = P(None, "data", None, None)
    weight_spec = P("stage", None, "data", None)
    return jax.shard_map(body, mesh=mesh, in_specs=(act_spec, act_spec, weight_spec, weight_spec, weight_spec), out_specs=(act_spec, weight_spec, weight_spec, weight_spec), check_vma=False)
```

time: 2220 us -> 1440 us (0.65)
  Pallas kernels: 2160 us -> 1380 us
    pallas_call x1, Pallas kernels: 2160 us -> 1380 us  [body(): pl.pallas_call(kernel, out_shape=outs, in_specs=[any_spec] * 5, out_specs...]
where the time goes in v2:
time: 1440 us; the launch traced here: 1430 us
  Pallas kernels  1380 us (96%)
  local copies, waits for them, and re-layouts  48.7 us (3%)
    pallas_call x1, Pallas kernels, body(): pl.pallas_call(kernel, out_shape=outs, in_specs=[any_spec] * 5, out_specs...  1380 us
    unnamed x16, local copies, waits for them, and re-layouts  48.7 us

profile of v2, /device:TPU:0, one launch (start us, length us, event | category | flops | bytes accessed | tf_op | source)
XLA Modules:
  0.0 1432.4 jit_solution(7677910871377878677)
XLA Ops:
  0.6 1383.1 %shard_map.84 = (bf16[4,2,64,2048]{3,2,1,0:T(8,128)(2,1)}, f32[2,512,5632]{2,1,0:T(8,128)}, f32[2,512,5632]{2,1,0:T(8,128)}, f32[2,1408,2048]{2,1,0:T(8,128)}, b...) custom-call(bf16[4,2,64,2048]{3,2,1,0:T(8,128)(2,1)} %bitcast.17, ...), custom_call_target="tpu_custom_call" | custom-call | tf_op jit(solution)/shard_map/pallas_call | solution.py:851
  1383.7 3.2 copy.13
  1386.9 0.0 slice-start
  1386.9 0.0 slice-start.1
  1386.9 0.0 slice-start.2
  1386.9 0.0 slice-start.3
  1386.9 18.7 %copy.14 = f32[1,2,512,5632]{3,2,1,0:T(8,128)} copy(f32[1,2,512,5632]{3,2,1,0:T(8,128)} %bitcast.13) | data formatting | bytes 46137344
  1405.6 0.0 slice-start.4
  1405.6 0.0 slice-start.5
  1405.6 18.6 %copy.15 = f32[1,2,512,5632]{3,2,1,0:T(8,128)} copy(f32[1,2,512,5632]{3,2,1,0:T(8,128)} %bitcast.12) | data formatting | bytes 46137344
  1424.1 0.0 slice-done
  1424.1 0.0 slice-done.1
  1424.1 0.0 slice-done.2
  1424.1 0.0 slice-done.3
  1424.2 0.0 slice-done.4
  1424.2 0.0 slice-done.5
  1424.2 8.2 copy.16
  (1 shorter events, 0.0 us)
Async XLA Ops:
  1386.9 37.3 %slice-start = ((s8[23068672]{0:T(1024)(128)(4,1)}), s8[4194304]{0:T(1024)(128)(4,1)S(1)}, s32[]{:S(2)}) async-start(s8[23068672]{0:T(1024)(128)(4,1)} %bitcast.9), calls=%async_computation | async-start | bytes 8388608
  1386.9 37.3 %slice-start.1 = ((s8[23068672]{0:T(1024)(128)(4,1)}), s8[4194304]{0:T(1024)(128)(4,1)S(1)}, s32[]{:S(2)}) async-start(s8[23068672]{0:T(1024)(128)(4,1)} %bitcast.9), calls=%async_computation.1 | async-start | bytes 8388608
  1386.9 37.3 %slice-start.2 = ((s8[23068672]{0:T(1024)(128)(4,1)}), s8[4194304]{0:T(1024)(128)(4,1)S(1)}, s32[]{:S(2)}) async-start(s8[23068672]{0:T(1024)(128)(4,1)} %bitcast.9), calls=%async_computation.2 | async-start | bytes 8388608
  1386.9 37.3 %slice-start.3 = ((s8[23068672]{0:T(1024)(128)(4,1)}), s8[4194304]{0:T(1024)(128)(4,1)S(1)}, s32[]{:S(2)}) async-start(s8[23068672]{0:T(1024)(128)(4,1)} %bitcast.9), calls=%async_computation.3 | async-start | bytes 8388608
  1405.6 18.6 %slice-start.4 = ((s8[23068672]{0:T(1024)(128)(4,1)}), s8[4194304]{0:T(1024)(128)(4,1)S(1)}, s32[]{:S(2)}) async-start(s8[23068672]{0:T(1024)(128)(4,1)} %bitcast.9), calls=%async_computation.4 | async-start | bytes 8388608
  1405.6 18.6 %slice-start.5 = ((s8[23068672]{0:T(1024)(128)(4,1)}), s8[2097152]{0:T(1024)(128)(4,1)S(1)}, s32[]{:S(2)}) async-start(s8[23068672]{0:T(1024)(128)(4,1)} %bitcast.9), calls=%async_computation.5 | async-start | bytes 4194304

commit v3 on v2

--- a/solution.py
+++ b/solution.py
@@ -29,7 +29,7 @@
 MS = 512
 
 
-(S_GU, S_O, S_OWN, S_TC, S_TB, S_NEAR, S_AB, S_COL, S_ST, S_ST1, S_AB1, S_FAR, S_SX, S_H, S_H1, S_H2, S_H3, S_HL) = range(18)
+(S_GU, S_O, S_OWN, S_TC, S_TB, S_NEAR, S_AB, S_COL, S_ST, S_ST1, S_AB1, S_FAR, S_SX, S_H, S_H1, S_H2, S_H3, S_HL, S_SPILL, S_SPILL2) = range(20)
 
 
 def mm(lhs, rhs, ld=1, rd=0):
@@ -57,9 +57,9 @@
 
 
 def kernel(x_ref, g_ref, wg_ref, wu_ref, wo_ref,
-           dx_ref, dwg_ref, dwu_ref, dwo_ref, WSP, WOS, WGU, WO, XALL, AB, RC, RB, WST, SX, H,
+           dx_ref, dwg_ref, dwu_ref, dwo_ref, WSP, WOS, WGU, WO, XALL, AB, RC, RB, WST, SX, H, DABH, SALH,
            gu, wo, nb, ab, dab, sall, part, two, tc, tb, hown, eown, nown, wst, ncol,
-           ls, w_spr, w_osr, w_t2r, w_br, w_ar, w_abr, w_or, w_s, w_os, ag_b, ag_a, ag_d, ag_c0, ag_c1, ag_s,
+           ls, w_spr, w_osr, w_t2r, w_br, w_ar, w_abr, w_or, w_s, w_os, ag_b, ag_a, ag_d, ag_c0, ag_c1, ag_s, ag_s2,
            rc_r, rc_s, rb_r, rb_s, g_b, g_c, g_o, g_bs, sx_r, sx_s, dx_r, dx_s):
     d = lax.axis_index("data")
     c = lax.axis_index("stage")
@@ -237,15 +237,22 @@
     def slot(ph, m, lo, n):
         return XALL.at[ph, m, pl.ds(lo * OWN, n * OWN)]
 
+    def lazy(ph):
+        return jnp.logical_or(ph == ONE, ph == TWO)
+
     def ag_start(ph, layer, m, src):
         an, bn = nbr(layer)
-        pltpu.make_async_copy(src, slot(ph, m, 0, 1), ls.at[S_OWN]).start()
+        pltpu.make_async_copy(src, slot(ph, m, 0, ONE), ls.at[S_OWN]).start()
         rcopy(src, slot(ph, m, ONE, ONE), ag_s.at[ph, m], ag_b.at[ph, m], (bn, c)).start()
-        rcopy(src, slot(ph, m, FAR, ONE), ag_s.at[ph, m], ag_a.at[ph, m], (an, c)).start()
-        wait_for(slot(ph, m, 0, 1), ls.at[S_OWN])
+
+        @pl.when(jnp.logical_not(lazy(ph)))
+        def _():
+            rcopy(src, slot(ph, m, FAR, ONE), ag_s.at[ph, m], ag_a.at[ph, m], (an, c)).start()
+
+        wait_for(slot(ph, m, 0, ONE), ls.at[S_OWN])
 
     def other_way(ph):
-        return jnp.logical_and(ph != 1, jnp.logical_or(ph < NL, ph >= NP - TWO))
+        return jnp.logical_or(jnp.logical_or(ph == 0, ph == LAST), jnp.logical_or(ph == NL + ONE, ph == NP - ONE))
 
     def ag_mid(ph, layer, m):
         an, bn = nbr(layer)
@@ -253,7 +260,7 @@
         wait_for(slot(ph, m, ONE, ONE), ag_b.at[ph, m])
         rcopy(slot(ph, m, 0, TWO), slot(ph, m, TWO, TWO), ag_s.at[ph, m], ag_c0.at[ph, m], mate).start()
 
-        @pl.when(jnp.logical_not(alt))
+        @pl.when(jnp.logical_not(jnp.logical_or(alt, lazy(ph))))
         def _():
             rcopy(slot(ph, m, ONE, ONE), slot(ph, m, FAR + ONE, ONE), ag_s.at[ph, m], ag_d.at[ph, m], (an, c)).start()
 
@@ -269,6 +276,16 @@
 
         wait_for(slot(ph, m, FAR + ONE, ONE), ag_d.at[ph, m])
         rcopy(slot(ph, m, FAR, TWO), slot(ph, m, FAR + TWO, TWO), ag_s.at[ph, m], ag_c1.at[ph, m], mate).start()
+
+    def far_start(ph, m):
+        an, bn = nbr(ph)
+        rcopy(slot(ph, m, 0, ONE), slot(ph, m, FAR, ONE), ag_s2.at[ph, m], ag_a.at[ph, m], (an, c)).start()
+        rcopy(slot(ph, m, ONE, ONE), slot(ph, m, FAR + ONE, ONE), ag_s2.at[ph, m], ag_d.at[ph, m], (an, c)).start()
+
+    def far_end(ph, m):
+        wait_for(slot(ph, m, FAR, ONE), ag_a.at[ph, m])
+        wait_for(slot(ph, m, FAR + ONE, ONE), ag_d.at[ph, m])
+        rcopy(slot(ph, m, FAR, TWO), slot(ph, m, FAR + TWO, TWO), ag_s2.at[ph, m], ag_c1.at[ph, m], mate).start()
 
     def ag_load(ph, m, half):
         wait_for(slot(ph, m, 2 + 4 * half, 2), (ag_c0, ag_c1)[half].at[ph, m])
@@ -279,7 +296,13 @@
         wait_for(nb.at[pl.ds(half * HALF, HALF)], ls.at[(S_NEAR, S_FAR)[half]])
 
     def ag_sent(ph, m):
-        wait_for(slot(ph, m, 0, 7), ag_s.at[ph, m])
+        @pl.when(lazy(ph))
+        def _():
+            wait_for(slot(ph, m, 0, LAST), ag_s.at[ph, m])
+
+        @pl.when(jnp.logical_not(lazy(ph)))
+        def _():
+            wait_for(slot(ph, m, 0, NS), ag_s.at[ph, m])
 
     def norm(h_rows):
         h_f = h_rows.astype(F32)
@@ -320,12 +343,16 @@
         def _():
             wait_for(two.at[m, pl.ds(OWN, OWN)], rb_s.at[ph - 1, m])
 
-    def pre(layer, m, half):
+    def pre(layer, m, half, store=True):
         rows = pl.ds(half * HALF, HALF)
-        ab[rows, :] = mm(nb[rows, :], gu[...])
-
-        @pl.when(layer < LAST)
-        def _():
+
+        def tile(i, carry):
+            some = pl.ds(pl.multiple_of(half * HALF + i * QUART, QUART), QUART)
+            ab[some, :] = mm(nb[some, :], gu[...])
+            return carry
+
+        lax.fori_loop(0, TWO, tile, 0)
+        if store:
             pltpu.make_async_copy(ab.at[rows], AB.at[layer, m, rows], ls.at[S_AB + 4 * half]).start()
 
     def ab_wait(half):
@@ -368,12 +395,16 @@
         nown[m] = n_f.astype(BF)
         ag_start(layer + 1, layer + 1, m, nown.at[m])
 
-    def b1(layer, m, half, loaded=False, between=None):
+    def b1(layer, m, half, between=None):
         rows = pl.ds(half * HALF, HALF)
         ag_loaded(half)
         t_buf = wst.at[half, :, pl.ds(0, FS)]
         t_buf[...] = mm(nb[rows, :], wo[...], ONE, ONE)
-        if not loaded:
+        if half:
+            @pl.when(jnp.logical_not(lazy(layer)))
+            def _():
+                ab_wait(half)
+        else:
             ab_wait(half)
         if between is not None:
             between()
@@ -399,10 +430,19 @@
                 dst = pl.ds(pl.multiple_of(m * ROWS + half * HALF + (1 - near) * 128, 128), QUART)
                 rcopy(sall.at[src, pl.ds(SPLIT, FS - SPLIT)], SX.at[layer, dst], sx_s.at[layer], sx_r.at[layer], mate).start()
 
-        if not loaded:
-            @pl.when(m < NM - 1)
-            def _():
-                pltpu.make_async_copy(AB.at[layer, m + 1, rows], ab.at[rows], ls.at[S_AB + 4 * half]).start()
+        @pl.when(layer > 0)
+        def _():
+            pltpu.make_async_copy(dab.at[into], DABH.at[layer - ONE, into], ls.at[S_SPILL]).start()
+            keep = pl.ds(0, SPLIT)
+            pltpu.make_async_copy(sall.at[into, keep], SALH.at[layer - ONE, into], ls.at[S_SPILL2]).start()
+
+        more = m < LAST
+        if half:
+            more = jnp.logical_and(more, jnp.logical_not(lazy(layer)))
+
+        @pl.when(more)
+        def _():
+            pltpu.make_async_copy(AB.at[layer, m + ONE, rows], ab.at[rows], ls.at[S_AB + 4 * half]).start()
 
     def b1_out(layer, m):
         ph = NS - ONE - layer
@@ -445,8 +485,9 @@
             pltpu.make_async_copy(XALL.at[layer, m, :, pl.ds(pl.multiple_of(which * MS, MS), MS)], ncol.at[pl.ds(m * ROWS, ROWS)], ls.at[S_COL]).start()
 
     def w_far(layer, i):
-        wst[i] = mm(ncol[:, pl.ds(i * HALF, HALF)], dab[...], 0, 0)
-        pltpu.make_async_copy(wst.at[i], WST.at[layer, pl.ds(i * HALF, HALF)], ls.at[S_ST + i]).start()
+        cols = pl.ds(pl.multiple_of(i * HALF, HALF), HALF)
+        wst[i] = mm(ncol[:, cols], dab[...], 0, 0)
+        pltpu.make_async_copy(wst.at[i], WST.at[layer, cols], ls.at[S_ST + i]).start()
 
     def w_send(layer, piece):
         p, k = home(layer)
@@ -466,7 +507,23 @@
 
         lax.fori_loop(lo, lo + n, step, 0)
 
-    def out_load(layer):
+    def spilled(layer):
+        wait_for(dab, ls.at[S_SPILL])
+        wait_for(SALH.at[0], ls.at[S_SPILL2])
+        x_sent(layer)
+
+    def x_sent(layer):
+        r, al, be = role(layer)
+
+        @pl.when(c == al)
+        def _():
+            wait_for(SX.at[layer], sx_s.at[layer])
+
+    def near_load(layer):
+        grad_cols(layer, d)
+        pltpu.make_async_copy(DABH.at[layer - ONE], dab, ls.at[S_SPILL]).start()
+
+    def out_load(layer, again):
         r, al, be = role(layer)
         for m in range(NM):
             pltpu.make_async_copy(XALL.at[NL + layer, m], gu.at[pl.ds(m * ROWS, ROWS), pl.ds(0, D)], ls.at[S_GU]).start()
@@ -476,13 +533,30 @@
             wait_for(SX.at[layer], sx_r.at[layer])
             pltpu.make_async_copy(SX.at[layer], sall.at[:, pl.ds(SPLIT, FS - SPLIT)], ls.at[S_SX]).start()
 
+        @pl.when(jnp.logical_and(again, c == al))
+        def _():
+            pltpu.make_async_copy(SALH.at[layer - ONE], sall.at[:, pl.ds(0, SPLIT)], ls.at[S_SX]).start()
+
+    def out_loaded(layer, again):
+        r, al, be = role(layer)
+        wait_for(gu.at[:, pl.ds(0, D)], ls.at[S_GU])
+
+        @pl.when(c != al)
+        def _():
+            wait_for(SX.at[layer], ls.at[S_SX])
+
+        @pl.when(jnp.logical_and(again, c == al))
+        def _():
+            wait_for(SALH.at[0], ls.at[S_SX])
+
     def w_near(layer, i):
         p, k = home(layer)
         r, al, be = role(layer)
-        wst[i] = mm(ncol[:, pl.ds(i * HALF, HALF)], dab[...], 0, 0)
+        cols = pl.ds(pl.multiple_of(i * HALF, HALF), HALF)
+        wst[i] = mm(ncol[:, cols], dab[...], 0, 0)
         for wi, ref in enumerate((dwg_ref, dwu_ref)):
             src = wst.at[i, :, pl.ds(wi * FS, FS)]
-            dst = ref.at[k, pl.ds(i * HALF, HALF), pl.ds(pl.multiple_of(chip(r, c, be) * FS, QUART), FS)]
+            dst = ref.at[k, cols, pl.ds(pl.multiple_of(chip(r, c, be) * FS, QUART), FS)]
 
             @pl.when(c == p)
             def _():
@@ -496,7 +570,7 @@
         for i in CORES:
             wait_for(wst.at[i], ls.at[S_ST + i])
 
-    def w_out(layer, tiles):
+    def w_out(layer):
         p, k = home(layer)
         r, al, be = role(layer)
         base = jnp.where(c == al, 0, SPLIT)
@@ -518,33 +592,29 @@
             def _():
                 rcopy(res, dst, ls.at[S_ST + slot], g_o.at[layer], (d, p)).start()
 
-        if 0 in tiles:
-            wait_for(gu.at[:, pl.ds(0, D)], ls.at[S_GU])
-
-            @pl.when(c != al)
-            def _():
-                wait_for(SX.at[layer], ls.at[S_SX])
-
-            def step(i, carry):
-                one(i, i, 256)
-                return carry
-
-            lax.fori_loop(0, 2, step, 0)
-        if 2 in tiles:
-            wait_for(rows_of(0, 256), ls.at[S_ST])
-
-            @pl.when(c == al)
-            def _():
-                one(2, 0, 256)
-                wait_for(rows_of(0, 256), ls.at[S_ST])
-                wait_for(SX.at[layer], sx_s.at[layer])
-
-            @pl.when(c != al)
-            def _():
-                one(2, 0, 128)
-                wait_for(rows_of(0, 128), ls.at[S_ST])
-
-            wait_for(rows_of(1, 256), ls.at[S_ST1])
+        def step(i, carry):
+            @pl.when(i == TWO)
+            def _():
+                wait_for(rows_of(0, HALF), ls.at[S_ST])
+
+            @pl.when(jnp.logical_or(i < TWO, c == al))
+            def _():
+                one(i, i % TWO, HALF)
+
+            return carry
+
+        lax.fori_loop(0, LAST, step, 0)
+
+        @pl.when(c == al)
+        def _():
+            wait_for(rows_of(0, HALF), ls.at[S_ST])
+
+        @pl.when(c != al)
+        def _():
+            one(TWO, 0, QUART)
+            wait_for(rows_of(0, QUART), ls.at[S_ST])
+
+        wait_for(rows_of(ONE, HALF), ls.at[S_ST1])
 
     w_core(0)
     for m in range(NM):
@@ -579,18 +649,15 @@
             load_gu(layer)
             wait_for(gu, ls.at[S_GU])
 
-        @pl.when(jnp.logical_and(t > 0, t < 13))
+        @pl.when(t > 0)
         def _():
             ab_wait(0)
 
-        @pl.when(t <= 12)
-        def _():
-            ag_load(layer, m, 0)
-
+        ag_load(layer, m, 0)
         ag_loaded(0)
         pre(layer, m, 0)
 
-        @pl.when(m == 0)
+        @pl.when(jnp.logical_and(m == 0, layer < LAST))
         def _():
             w_wait_o(layer)
             load_o(layer)
@@ -600,10 +667,6 @@
         def _():
             f1_out(layer, m)
 
-        @pl.when(layer == LAST)
-        def _():
-            ag_load(NL + layer, m, 0)
-
         @pl.when(jnp.logical_and(t >= 2, t < 14))
         def _():
             f3((t - 2) // NM, (t - 2) % NM)
@@ -612,42 +675,22 @@
         def _():
             ag_mid((t - 3) // NM + 1, (t - 3) // NM + 1, (t - 3) % NM)
 
-        ag_end(layer, m)
-
-        @pl.when(jnp.logical_and(t > 0, t < 13))
-        def _():
-            ab_wait(1)
-
-        ag_load(layer, m, 1)
-
-        @pl.when(layer == LAST)
-        def _():
-            b1(layer, m, 0, True)
-            b1_out(layer, m)
-
-            @pl.when(m < NM - 1)
-            def _():
-                ag_load(layer, m + 1, 0)
-
-        ag_loaded(1)
-        pre(layer, m, 1)
+        @pl.when(jnp.logical_not(lazy(layer)))
+        def _():
+            ag_end(layer, m)
+
+            @pl.when(t > 0)
+            def _():
+                ab_wait(ONE)
+
+            ag_load(layer, m, ONE)
+            ag_loaded(ONE)
+            pre(layer, m, ONE)
 
         @pl.when(layer < LAST)
         def _():
             rs_load(layer, m)
             rs_split(layer, layer, m)
-
-        @pl.when(layer == LAST)
-        def _():
-            ag_load(NL + layer, m, 1)
-
-            @pl.when(m >= 2)
-            def _():
-                rs_total_load(NS - ONE - layer, m - 2)
-                b3(layer, m - 2)
-
-            b1(layer, m, 1, True, lambda: rs_load(NS - ONE - layer, m))
-            rs_split(NS - ONE - layer, layer, m)
 
         def at(step, *work):
             @pl.when(t == step)
@@ -660,7 +703,7 @@
                 fn(NP - ONE, LAST, m_)
 
         plan = ("F1a P2a", "F1bc P2b", "F1d S2a P2c", "S2bcd P2d", "P3ab F2a", "F2bcd P3cd D2a",
-                "D2bcd D3ab", "S3abcd D3cd", "", "F3a", "F3b", "F3cd")
+                "D2bcd D3a", "S3abcd D3b", "F3a", "F3b", "F3cd D3c", "D3d")
         sends = {"F": w_fwd, "P": w_pair, "S": w_split, "D": w_down}
         for step, words in enumerate(plan):
             for w in words.split():
@@ -669,40 +712,40 @@
         at(7, lambda: each(lambda ph, l, m_: ag_start(ph, l, m_, eown.at[m_])))
         at(9, lambda: each(ag_mid))
         at(11, lambda: each(lambda ph, l, m_: ag_end(ph, m_)))
+
+        @pl.when(layer == LAST)
+        def _():
+            far_start(TWO, m)
+            far_start(ONE, m)
+
         return carry
 
     lax.fori_loop(0, NL * NM, fwd_step, 0)
+    ab_wait(0)
+    ab_wait(1)
+    w_wait_o(LAST)
 
     def bwd_layer(i, carry):
         layer = LAST - i
+        up = layer + ONE
         ph = NS - ONE - layer
         an, bn = nbr(layer)
-        grad_cols(layer, bn)
+        late = lazy(layer)
+        near = pl.ds(0, HALF)
+        far = pl.ds(HALF, HALF)
+        pltpu.make_async_copy(AB.at[layer, 0, near], ab.at[near], ls.at[S_AB]).start()
+
+        @pl.when(jnp.logical_not(late))
+        def _():
+            pltpu.make_async_copy(AB.at[layer, 0, far], ab.at[far], ls.at[S_AB1]).start()
+
+        load_o(layer)
 
         @pl.when(layer < LAST)
         def _():
-            for half in CORES:
-                rows = pl.ds(half * HALF, HALF)
-                pltpu.make_async_copy(AB.at[layer, 0, rows], ab.at[rows], ls.at[S_AB + 4 * half]).start()
-            load_o(layer)
             load_gu(layer)
 
-            @pl.when(layer > 0)
-            def _():
-                pltpu.make_async_copy(H.at[layer - 1], hown, ls.at[S_HL]).start()
-
-            @pl.when(layer == 0)
-            def _():
-                for m in range(NM):
-                    pltpu.make_async_copy(x_ref.at[m, c], hown.at[m], ls.at[S_HL]).start()
-
-            wait_for(wo, ls.at[S_O])
-            wait_for(hown, ls.at[S_HL])
-
-        def gather_mid(m):
-            @pl.when(layer > 0)
-            def _():
-                ag_mid(NL - ONE + layer, layer - 1, m)
+        wait_for(wo, ls.at[S_O])
 
         def bulk(lyr, at, n, *only):
             for v in only:
@@ -710,89 +753,157 @@
                 def _():
                     w_sends(lyr, at, n)
 
-        bulk(3, 4, 1, 2)
-        bulk(3, 13, 3, 1)
-        bulk(2, 0, 1, 1)
-        bulk(2, 11, 5, 0)
-        bulk(1, 0, 4, 0)
+        ag_load(NL + layer, 0, 0)
+
+        @pl.when(layer < LAST)
+        def _():
+            spilled(up)
 
         def step(m, c2):
-            ag_load(NL + layer, m, 1)
+            first = jnp.logical_and(m == 0, layer < LAST)
+            ag_load(jnp.where(late, layer, NL + layer), m, ONE)
+
+            @pl.when(m == LAST)
+            def _():
+                grad_cols(layer, bn)
+
             b1(layer, m, 0)
 
-            @pl.when(m >= 2)
-            def _():
-                rs_total_load(ph, m - 2)
+            @pl.when(m >= TWO)
+            def _():
+                rs_total_load(ph, m - TWO)
+
+            @pl.when(first)
+            def _():
+                rs_total_load(ph - ONE, NM - ONE)
 
             b1_out(layer, m)
 
-            @pl.when(m < NM - 1)
-            def _():
-                ag_end(NL + layer, m + 1)
-                ag_load(NL + layer, m + 1, 0)
-
-            @pl.when(m >= 2)
-            def _():
-                b3(layer, m - 2)
-
-            bulk(3, 5 + 2 * m, 1, 2)
-            bulk(2, 1 + 2 * m, 1, 1)
-            b1(layer, m, 1, False, lambda: rs_load(ph, m))
+            @pl.when(late)
+            def _():
+                ag_loaded(ONE)
+                pre(layer, m, ONE, False)
+                ag_load(NL + layer, m, ONE)
+
+            @pl.when(first)
+            def _():
+                b3(up, NM - ONE)
+                ag_mid(NL + layer, layer, TWO)
+
+                @pl.when(layer > 0)
+                def _():
+                    pltpu.make_async_copy(H.at[layer - ONE], hown, ls.at[S_HL]).start()
+
+                @pl.when(layer == 0)
+                def _():
+                    for mm_ in range(NM):
+                        pltpu.make_async_copy(x_ref.at[mm_, c], hown.at[mm_], ls.at[S_HL]).start()
+
+                wait_for(hown, ls.at[S_HL])
+
+            @pl.when(jnp.logical_and(m == ONE, layer < LAST))
+            def _():
+                ag_mid(NL + layer, layer, NM - ONE)
+
+            @pl.when(m < NM - ONE)
+            def _():
+                @pl.when(layer < LAST)
+                def _():
+                    ag_end(NL + layer, m + ONE)
+
+                ag_load(NL + layer, m + ONE, 0)
+
+            @pl.when(m >= TWO)
+            def _():
+                b3(layer, m - TWO)
+
+            bulk(LAST, m, ONE, TWO)
+            bulk(TWO, TWO * m, TWO, ONE)
+            bulk(LAST, NM + TWO * m, TWO, 0)
+            bulk(TWO, NP + m, ONE, 0)
+            b1(layer, m, ONE, lambda: rs_load(ph, m))
             rs_split(ph, layer, m)
-            bulk(3, 6 + 2 * m, 1, 2)
-            bulk(2, 2 + 2 * m, 1, 1)
-            bulk(1, 4 + 3 * m, 3, 0)
             return c2
 
-        @pl.when(layer < LAST)
-        def _():
-            ag_load(NL + layer, 0, 0)
-            lax.fori_loop(0, NM, step, 0)
-
-        out_load(layer)
+        lax.fori_loop(0, NM, step, 0)
         wait_for(ncol, ls.at[S_COL])
-        w_far(layer, 0)
-        rs_total_load(ph, 2)
-        w_far(layer, 1)
-        b3(layer, 2)
-        grad_cols(layer, d)
+
+        def far_tile(i, c2):
+            w_far(layer, i)
+
+            @pl.when(i == 0)
+            def _():
+                rs_total_load(ph, TWO)
+
+                @pl.when(layer > 0)
+                def _():
+                    ag_mid(LAST + layer, layer - ONE, 0)
+
+            return c2
+
+        lax.fori_loop(0, TWO, far_tile, 0)
+        b3(layer, TWO)
         near_end()
 
-        @pl.when(layer == 0)
-        def _():
-            w_sends(0, 0, 16)
-
-        gather_mid(0)
+        @pl.when(layer > 0)
+        def _():
+            ag_mid(LAST + layer, layer - ONE, ONE)
+            ag_end(LAST + layer, 0)
+
+        @pl.when(jnp.logical_and(layer > ONE, layer < NL))
+        def _():
+            for m in range(NM):
+                far_end(layer - ONE, m)
+
+        return carry
+
+    lax.fori_loop(0, NL, bwd_layer, 0)
+
+    w_sends(0, 0, NP + NP)
+    w_sends(LAST, NM + NP, NM)
+    w_sends(ONE, 0, NP + NP)
+    w_sends(TWO, NM + NP, NM)
+    grad_cols(0, d)
+    x_sent(0)
+    rs_total_load(NS - ONE, LAST)
+
+    def rest(i, carry):
+        layer = (NL - i) % NL
+        again = i > 0
+        out_load(layer, again)
         wait_for(ncol, ls.at[S_COL])
-        w_near(layer, 0)
-        rs_total_load(ph, 3)
-        b3(layer, 3)
-        bulk(3, 0, 1, 3)
-        w_near(layer, 1)
-        bulk(3, 1, 1, 3)
-        gather_mid(1)
+
+        @pl.when(again)
+        def _():
+            wait_for(dab, ls.at[S_SPILL])
+
+        def near_tile(j, c2):
+            w_near(layer, j)
+            return c2
+
+        lax.fori_loop(0, TWO, near_tile, 0)
+
+        @pl.when(i == 0)
+        def _():
+            b3(0, LAST)
+
+        @pl.when(i < LAST)
+        def _():
+            near_load(LAST - i)
+
         near_end()
-        w_out(layer, (0, 1))
-        bulk(3, 2, 1, 3)
-        bulk(2, 9, 1, 1)
-        gather_mid(2)
-        w_out(layer, (2,))
-        bulk(3, 3, 1, 3)
-        bulk(2, 10, 1, 1)
-        gather_mid(3)
-
-        @pl.when(layer > 0)
-        def _():
-            ag_end(NL - ONE + layer, 0)
-
+        out_loaded(layer, again)
+        w_out(layer)
         return carry
 
-    lax.fori_loop(0, NL, bwd_layer, 0)
+    lax.fori_loop(0, NL, rest, 0)
 
     for m in range(NM):
         wait_for(dx_ref.at[m, 1 - c], dx_r.at[m])
         wait_for(dx_ref.at[m, c], dx_s.at[m])
-        ag_sent(3, m)
+        ag_sent(LAST, m)
+        for ph in (ONE, TWO):
+            wait_for(slot(ph, m, 0, FAR), ag_s2.at[ph, m])
         wait_for(two.at[m, pl.ds(OWN, OWN)], rb_s.at[6, m])
     wait_for(part, rc_s.at[6, NM - 1])
     for l in range(NL):
@@ -838,14 +949,15 @@
             hbm((NM, 2, OWN, D), BF), hbm((2, MS, 4 * FS), F32), hbm((2, MS, 4 * FS), F32), hbm((2, FS, D), F32),
             hbm((NL, MS, F2C), BF), hbm((NL, FS // 2, D), BF),
             hbm((NL, D, F2C), BF), hbm((NL, FS, D), BF), hbm((NP, NM, ROWS, D), BF), hbm((NL, NM, ROWS, F2C), F32),
-            hbm((NS, NM, QUART, D), F32), hbm((NS, NM, OWN, D), F32), hbm((NL, MS, F2C), F32), hbm((NL, NM * ROWS, FS - SPLIT), BF), hbm((2, NM, OWN, D), BF))
+            hbm((NS, NM, QUART, D), F32), hbm((NS, NM, OWN, D), F32), hbm((NL, MS, F2C), F32), hbm((NL, NM * ROWS, FS - SPLIT), BF), hbm((2, NM, OWN, D), BF),
+            hbm((LAST, NM * ROWS, F2C), BF), hbm((LAST, NM * ROWS, SPLIT), BF))
         scratch = [
             pltpu.VMEM((D, F2C), BF), pltpu.VMEM((FS, D), BF), pltpu.VMEM((ROWS, D), BF), pltpu.VMEM((ROWS, F2C), F32),
             pltpu.VMEM((NM * ROWS, F2C), BF), pltpu.VMEM((NM * ROWS, FS), BF), pltpu.VMEM((QUART, D), F32),
             pltpu.VMEM((NM, QUART, D), F32), pltpu.VMEM((QUART, D), F32), pltpu.VMEM((OWN, D), F32),
             pltpu.VMEM((NM, OWN, D), BF), pltpu.VMEM((NM, OWN, D), BF), pltpu.VMEM((NM, OWN, D), BF), pltpu.VMEM((2, 256, F2C), F32), pltpu.VMEM((NM * ROWS, MS), BF),
-            dma((S_HL + ONE,)), dma((NL,)), dma((NL,)), dma((NL,)), dma((NL, 2, 2)), dma((NL,)), dma((NL,)), dma((NL,)), dma((NL, 4)), dma((NL, 3)),
-            dma((NP, NM)), dma((NP, NM)), dma((NP, NM)), dma((NP, NM)), dma((NP, NM)), dma((NP, NM)),
+            dma((S_SPILL2 + ONE,)), dma((NL,)), dma((NL,)), dma((NL,)), dma((NL, 2, 2)), dma((NL,)), dma((NL,)), dma((NL,)), dma((NL, 4)), dma((NL, 3)),
+            dma((NP, NM)), dma((NP, NM)), dma((NP, NM)), dma((NP, NM)), dma((NP, NM)), dma((NP, NM)), dma((NP, NM)),
             dma((NS, NM)), dma((NS, NM)), dma((NS, NM)), dma((NS, NM)), dma((NL,)), dma((NL,)), dma((NL,)), dma((NL,)), dma((NL,)), dma((NL,)),
             dma((NM,)), dma((NM,))]
         res = pl.pallas_call(

time: 1440 us -> 1330 us (0.924)
  Pallas kernels: 1380 us -> 1280 us
    pallas_call x1, Pallas kernels: 1380 us -> 1280 us  [body(): pl.pallas_call(kernel, out_shape=outs, in_specs=[any_spec] * 5, out_specs...]
where the time goes in v3:
time: 1330 us
  Pallas kernels  1280 us (96%)
  local copies, waits for them, and re-layouts  48.7 us (4%)
    pallas_call x1, Pallas kernels, body(): pl.pallas_call(kernel, out_shape=outs, in_specs=[any_spec] * 5, out_specs...  1280 us
    unnamed x16, local copies, waits for them, and re-layouts  48.7 us

profile of v3, /device:TPU:0, one launch (start us, length us, event | category | flops | bytes accessed | tf_op | source)
XLA Modules:
  0.0 1327.6 jit_solution(14103988097567403886)
XLA Ops:
  0.6 1278.3 %shard_map.84 = (bf16[4,2,64,2048]{3,2,1,0:T(8,128)(2,1)}, f32[2,512,5632]{2,1,0:T(8,128)}, f32[2,512,5632]{2,1,0:T(8,128)}, f32[2,1408,2048]{2,1,0:T(8,128)}, b...) custom-call(bf16[4,2,64,2048]{3,2,1,0:T(8,128)(2,1)} %bitcast.17, ...), custom_call_target="tpu_custom_call" | custom-call | tf_op jit(solution)/shard_map/pallas_call | solution.py:963
  1278.9 3.2 copy.13
  1282.1 0.0 slice-start
  1282.1 0.0 slice-start.1
  1282.1 0.0 slice-start.2
  1282.1 0.0 slice-start.3
  1282.1 18.7 %copy.14 = f32[1,2,512,5632]{3,2,1,0:T(8,128)} copy(f32[1,2,512,5632]{3,2,1,0:T(8,128)} %bitcast.13) | data formatting | bytes 46137344
  1300.8 0.0 slice-start.4
  1300.8 0.0 slice-start.5
  1300.8 18.6 %copy.15 = f32[1,2,512,5632]{3,2,1,0:T(8,128)} copy(f32[1,2,512,5632]{3,2,1,0:T(8,128)} %bitcast.12) | data formatting | bytes 46137344
  1319.3 0.0 slice-done
  1319.3 0.0 slice-done.1
  1319.4 0.0 slice-done.2
  1319.4 0.0 slice-done.3
  1319.4 0.0 slice-done.4
  1319.4 0.0 slice-done.5
  1319.4 8.2 copy.16
  (1 shorter events, 0.0 us)
Async XLA Ops:
  1282.1 37.3 %slice-start = ((s8[23068672]{0:T(1024)(128)(4,1)}), s8[4194304]{0:T(1024)(128)(4,1)S(1)}, s32[]{:S(2)}) async-start(s8[23068672]{0:T(1024)(128)(4,1)} %bitcast.9), calls=%async_computation | async-start | bytes 8388608
  1282.1 37.3 %slice-start.1 = ((s8[23068672]{0:T(1024)(128)(4,1)}), s8[4194304]{0:T(1024)(128)(4,1)S(1)}, s32[]{:S(2)}) async-start(s8[23068672]{0:T(1024)(128)(4,1)} %bitcast.9), calls=%async_computation.1 | async-start | bytes 8388608
  1282.1 37.3 %slice-start.2 = ((s8[23068672]{0:T(1024)(128)(4,1)}), s8[4194304]{0:T(1024)(128)(4,1)S(1)}, s32[]{:S(2)}) async-start(s8[23068672]{0:T(1024)(128)(4,1)} %bitcast.9), calls=%async_computation.2 | async-start | bytes 8388608
  1282.1 37.3 %slice-start.3 = ((s8[23068672]{0:T(1024)(128)(4,1)}), s8[4194304]{0:T(1024)(128)(4,1)S(1)}, s32[]{:S(2)}) async-start(s8[23068672]{0:T(1024)(128)(4,1)} %bitcast.9), calls=%async_computation.3 | async-start | bytes 8388608
  1300.8 18.6 %slice-start.4 = ((s8[23068672]{0:T(1024)(128)(4,1)}), s8[4194304]{0:T(1024)(128)(4,1)S(1)}, s32[]{:S(2)}) async-start(s8[23068672]{0:T(1024)(128)(4,1)} %bitcast.9), calls=%async_computation.4 | async-start | bytes 8388608
  1300.8 18.6 %slice-start.5 = ((s8[23068672]{0:T(1024)(128)(4,1)}), s8[2097152]{0:T(1024)(128)(4,1)S(1)}, s32[]{:S(2)}) async-start(s8[23068672]{0:T(1024)(128)(4,1)} %bitcast.9), calls=%async_computation.5 | async-start | bytes 4194304

commit v4 on v3

--- a/solution.py
+++ b/solution.py
@@ -252,7 +252,7 @@
         wait_for(slot(ph, m, 0, ONE), ls.at[S_OWN])
 
     def other_way(ph):
-        return jnp.logical_or(jnp.logical_or(ph == 0, ph == LAST), jnp.logical_or(ph == NL + ONE, ph == NP - ONE))
+        return jnp.logical_or(jnp.logical_or(ph == 0, ph == LAST), ph > NL)
 
     def ag_mid(ph, layer, m):
         an, bn = nbr(layer)
@@ -400,12 +400,12 @@
         ag_loaded(half)
         t_buf = wst.at[half, :, pl.ds(0, FS)]
         t_buf[...] = mm(nb[rows, :], wo[...], ONE, ONE)
-        if half:
-            @pl.when(jnp.logical_not(lazy(layer)))
-            def _():
-                ab_wait(half)
-        else:
+        kept = layer < LAST if half == 0 else layer == 0
+
+        @pl.when(kept)
+        def _():
             ab_wait(half)
+
         if between is not None:
             between()
         into = pl.ds(pl.multiple_of(m * ROWS + half * HALF, HALF), 256)
@@ -436,11 +436,7 @@
             keep = pl.ds(0, SPLIT)
             pltpu.make_async_copy(sall.at[into, keep], SALH.at[layer - ONE, into], ls.at[S_SPILL2]).start()
 
-        more = m < LAST
-        if half:
-            more = jnp.logical_and(more, jnp.logical_not(lazy(layer)))
-
-        @pl.when(more)
+        @pl.when(jnp.logical_and(m < LAST, kept))
         def _():
             pltpu.make_async_copy(AB.at[layer, m + ONE, rows], ab.at[rows], ls.at[S_AB + 4 * half]).start()
 
@@ -703,7 +699,7 @@
                 fn(NP - ONE, LAST, m_)
 
         plan = ("F1a P2a", "F1bc P2b", "F1d S2a P2c", "S2bcd P2d", "P3ab F2a", "F2bcd P3cd D2a",
-                "D2bcd D3a", "S3abcd D3b", "F3a", "F3b", "F3cd D3c", "D3d")
+                "D2bcd D3ab", "S3abcd D3cd", "F3a", "F3b", "F3cd")
         sends = {"F": w_fwd, "P": w_pair, "S": w_split, "D": w_down}
         for step, words in enumerate(plan):
             for w in words.split():
@@ -713,39 +709,38 @@
         at(9, lambda: each(ag_mid))
         at(11, lambda: each(lambda ph, l, m_: ag_end(ph, m_)))
 
-        @pl.when(layer == LAST)
-        def _():
-            far_start(TWO, m)
-            far_start(ONE, m)
-
         return carry
 
-    lax.fori_loop(0, NL * NM, fwd_step, 0)
+    lax.fori_loop(0, LAST * NM, fwd_step, 0)
     ab_wait(0)
-    ab_wait(1)
+    ab_wait(ONE)
+    w_wait_gu(LAST)
+    load_gu(LAST)
     w_wait_o(LAST)
+    wait_for(gu, ls.at[S_GU])
+
+    def layer_loads(layer):
+        near = pl.ds(0, HALF)
+        far = pl.ds(HALF, HALF)
+        load_o(layer)
+
+        @pl.when(layer < LAST)
+        def _():
+            pltpu.make_async_copy(AB.at[layer, 0, near], ab.at[near], ls.at[S_AB]).start()
+            load_gu(layer)
+
+        @pl.when(layer == 0)
+        def _():
+            pltpu.make_async_copy(AB.at[layer, 0, far], ab.at[far], ls.at[S_AB1]).start()
+
+    layer_loads(LAST)
 
     def bwd_layer(i, carry):
         layer = LAST - i
         up = layer + ONE
         ph = NS - ONE - layer
         an, bn = nbr(layer)
-        late = lazy(layer)
-        near = pl.ds(0, HALF)
-        far = pl.ds(HALF, HALF)
-        pltpu.make_async_copy(AB.at[layer, 0, near], ab.at[near], ls.at[S_AB]).start()
-
-        @pl.when(jnp.logical_not(late))
-        def _():
-            pltpu.make_async_copy(AB.at[layer, 0, far], ab.at[far], ls.at[S_AB1]).start()
-
-        load_o(layer)
-
-        @pl.when(layer < LAST)
-        def _():
-            load_gu(layer)
-
-        wait_for(wo, ls.at[S_O])
+        late = layer > 0
 
         def bulk(lyr, at, n, *only):
             for v in only:
@@ -753,19 +748,39 @@
                 def _():
                     w_sends(lyr, at, n)
 
-        ag_load(NL + layer, 0, 0)
+        wait_for(wo, ls.at[S_O])
 
         @pl.when(layer < LAST)
         def _():
+            ag_load(NL + layer, 0, 0)
             spilled(up)
 
         def step(m, c2):
             first = jnp.logical_and(m == 0, layer < LAST)
-            ag_load(jnp.where(late, layer, NL + layer), m, ONE)
-
-            @pl.when(m == LAST)
-            def _():
-                grad_cols(layer, bn)
+            early = jnp.logical_or(m > 0, layer == LAST)
+
+            @pl.when(layer == LAST)
+            def _():
+                ag_load(layer, m, 0)
+                ag_loaded(0)
+                pre(layer, m, 0, False)
+                ag_load(NL + layer, m, 0)
+
+                @pl.when(m < TWO)
+                def _():
+                    f3(TWO, m + TWO)
+
+                @pl.when(m < LAST)
+                def _():
+                    ag_mid(LAST, LAST, m + ONE)
+
+            @pl.when(lazy(layer))
+            def _():
+                ag_load(layer, m, ONE)
+
+            @pl.when(jnp.logical_and(jnp.logical_not(late), early))
+            def _():
+                ag_load(NL + layer, m, ONE)
 
             b1(layer, m, 0)
 
@@ -778,12 +793,29 @@
                 rs_total_load(ph - ONE, NM - ONE)
 
             b1_out(layer, m)
+
+            @pl.when(jnp.logical_not(early))
+            def _():
+                ag_end(NL + layer, 0)
+
+            @pl.when(layer == LAST)
+            def _():
+                ag_end(layer, m)
+                ag_load(layer, m, ONE)
 
             @pl.when(late)
             def _():
                 ag_loaded(ONE)
                 pre(layer, m, ONE, False)
                 ag_load(NL + layer, m, ONE)
+
+            @pl.when(jnp.logical_and(jnp.logical_not(late), jnp.logical_not(early)))
+            def _():
+                ag_load(NL + layer, m, ONE)
+
+            @pl.when(m == LAST)
+            def _():
+                grad_cols(layer, bn)
 
             @pl.when(first)
             def _():
@@ -805,27 +837,35 @@
             def _():
                 ag_mid(NL + layer, layer, NM - ONE)
 
-            @pl.when(m < NM - ONE)
-            def _():
-                @pl.when(layer < LAST)
-                def _():
-                    ag_end(NL + layer, m + ONE)
-
+            @pl.when(jnp.logical_and(m < LAST, layer < LAST))
+            def _():
+                ag_end(NL + layer, m + ONE)
                 ag_load(NL + layer, m + ONE, 0)
 
             @pl.when(m >= TWO)
             def _():
                 b3(layer, m - TWO)
 
-            bulk(LAST, m, ONE, TWO)
-            bulk(TWO, TWO * m, TWO, ONE)
-            bulk(LAST, NM + TWO * m, TWO, 0)
-            bulk(TWO, NP + m, ONE, 0)
+            bulk(LAST, 1 + 1 * m, 1, TWO)
+            bulk(TWO, 1 + 2 * m, 2, ONE)
+            bulk(LAST, 5 + 2 * m, 2, 0)
+            bulk(TWO, 9 + 1 * m, 1, 0)
             b1(layer, m, ONE, lambda: rs_load(ph, m))
             rs_split(ph, layer, m)
+
+            @pl.when(layer == LAST)
+            def _():
+                far_start(TWO, m)
+                far_start(ONE, m)
+
             return c2
 
         lax.fori_loop(0, NM, step, 0)
+
+        @pl.when(layer > 0)
+        def _():
+            layer_loads(layer - ONE)
+
         wait_for(ncol, ls.at[S_COL])
 
         def far_tile(i, c2):
@@ -848,7 +888,10 @@
         @pl.when(layer > 0)
         def _():
             ag_mid(LAST + layer, layer - ONE, ONE)
-            ag_end(LAST + layer, 0)
+
+        bulk(3, 0, 1, 3)
+        bulk(2, 0, 1, 2)
+        bulk(1, 0, 1, 1)
 
         @pl.when(jnp.logical_and(layer > ONE, layer < NL))
         def _():
@@ -860,9 +903,9 @@
     lax.fori_loop(0, NL, bwd_layer, 0)
 
     w_sends(0, 0, NP + NP)
-    w_sends(LAST, NM + NP, NM)
-    w_sends(ONE, 0, NP + NP)
-    w_sends(TWO, NM + NP, NM)
+    w_sends(LAST, 13, 3)
+    w_sends(ONE, 1, 15)
+    w_sends(TWO, 13, 3)
     grad_cols(0, d)
     x_sent(0)
     rs_total_load(NS - ONE, LAST)

time: 1330 us -> 1300 us (0.977)
  Pallas kernels: 1280 us -> 1240 us
    pallas_call x1, Pallas kernels: 1280 us -> 1240 us  [body(): pl.pallas_call(kernel, out_shape=outs, in_specs=[any_spec] * 5, out_specs...]
where the time goes in v4:
time: 1300 us; the launch traced here: 1290 us
  Pallas kernels  1240 us (95%)
  local copies, waits for them, and re-layouts  48.7 us (4%)
    pallas_call x1, Pallas kernels, body(): pl.pallas_call(kernel, out_shape=outs, in_specs=[any_spec] * 5, out_specs...  1240 us
    unnamed x16, local copies, waits for them, and re-layouts  48.7 us

profile of v4, /device:TPU:0, one launch (start us, length us, event | category | flops | bytes accessed | tf_op | source)
XLA Modules:
  0.0 1294.1 jit_solution(17368106713885089687)
XLA Ops:
  0.6 1244.7 %shard_map.84 = (bf16[4,2,64,2048]{3,2,1,0:T(8,128)(2,1)}, f32[2,512,5632]{2,1,0:T(8,128)}, f32[2,512,5632]{2,1,0:T(8,128)}, f32[2,1408,2048]{2,1,0:T(8,128)}, b...) custom-call(bf16[4,2,64,2048]{3,2,1,0:T(8,128)(2,1)} %bitcast.17, ...), custom_call_target="tpu_custom_call" | custom-call | tf_op jit(solution)/shard_map/pallas_call | solution.py:1006
  1245.4 3.2 copy.13
  1248.5 0.0 slice-start
  1248.5 0.0 slice-start.1
  1248.5 0.0 slice-start.2
  1248.5 0.0 slice-start.3
  1248.6 18.7 %copy.14 = f32[1,2,512,5632]{3,2,1,0:T(8,128)} copy(f32[1,2,512,5632]{3,2,1,0:T(8,128)} %bitcast.13) | data formatting | bytes 46137344
  1267.3 0.0 slice-start.4
  1267.3 0.0 slice-start.5
  1267.3 18.6 %copy.15 = f32[1,2,512,5632]{3,2,1,0:T(8,128)} copy(f32[1,2,512,5632]{3,2,1,0:T(8,128)} %bitcast.12) | data formatting | bytes 46137344
  1285.8 0.0 slice-done
  1285.8 0.0 slice-done.1
  1285.8 0.0 slice-done.2
  1285.8 0.0 slice-done.3
  1285.8 0.0 slice-done.4
  1285.9 0.0 slice-done.5
  1285.9 8.2 copy.16
  (1 shorter events, 0.0 us)
Async XLA Ops:
  1248.5 37.3 %slice-start = ((s8[23068672]{0:T(1024)(128)(4,1)}), s8[4194304]{0:T(1024)(128)(4,1)S(1)}, s32[]{:S(2)}) async-start(s8[23068672]{0:T(1024)(128)(4,1)} %bitcast.9), calls=%async_computation | async-start | bytes 8388608
  1248.5 37.3 %slice-start.1 = ((s8[23068672]{0:T(1024)(128)(4,1)}), s8[4194304]{0:T(1024)(128)(4,1)S(1)}, s32[]{:S(2)}) async-start(s8[23068672]{0:T(1024)(128)(4,1)} %bitcast.9), calls=%async_computation.1 | async-start | bytes 8388608
  1248.5 37.3 %slice-start.2 = ((s8[23068672]{0:T(1024)(128)(4,1)}), s8[4194304]{0:T(1024)(128)(4,1)S(1)}, s32[]{:S(2)}) async-start(s8[23068672]{0:T(1024)(128)(4,1)} %bitcast.9), calls=%async_computation.2 | async-start | bytes 8388608
  1248.5 37.3 %slice-start.3 = ((s8[23068672]{0:T(1024)(128)(4,1)}), s8[4194304]{0:T(1024)(128)(4,1)S(1)}, s32[]{:S(2)}) async-start(s8[23068672]{0:T(1024)(128)(4,1)} %bitcast.9), calls=%async_computation.3 | async-start | bytes 8388608
  1267.3 18.6 %slice-start.4 = ((s8[23068672]{0:T(1024)(128)(4,1)}), s8[4194304]{0:T(1024)(128)(4,1)S(1)}, s32[]{:S(2)}) async-start(s8[23068672]{0:T(1024)(128)(4,1)} %bitcast.9), calls=%async_computation.4 | async-start | bytes 8388608
  1267.3 18.6 %slice-start.5 = ((s8[23068672]{0:T(1024)(128)(4,1)}), s8[2097152]{0:T(1024)(128)(4,1)S(1)}, s32[]{:S(2)}) async-start(s8[23068672]{0:T(1024)(128)(4,1)} %bitcast.9), calls=%async_computation.5 | async-start | bytes 4194304

commit v5 on v4

--- a/solution.py
+++ b/solution.py
@@ -48,6 +48,9 @@
         body(full * tile, total % tile)
 
 
+OUT_T = 13
+
+
 def flip(v):
     return ONE - v
 
@@ -57,7 +60,7 @@
 
 
 def kernel(x_ref, g_ref, wg_ref, wu_ref, wo_ref,
-           dx_ref, dwg_ref, dwu_ref, dwo_ref, WSP, WOS, WGU, WO, XALL, AB, RC, RB, WST, SX, H, DABH, SALH,
+           dx_ref, dwg_ref, dwu_ref, dwo_ref, WSP, WOS, WGU, WO, XALL, AB, RC, RB, WST, WT0, WT1, SX, H, DABH, SALH,
            gu, wo, nb, ab, dab, sall, part, two, tc, tb, hown, eown, nown, wst, ncol,
            ls, w_spr, w_osr, w_t2r, w_br, w_ar, w_abr, w_or, w_s, w_os, ag_b, ag_a, ag_d, ag_c0, ag_c1, ag_s, ag_s2,
            rc_r, rc_s, rb_r, rb_s, g_b, g_c, g_o, g_bs, sx_r, sx_s, dx_r, dx_s):
@@ -483,7 +486,16 @@
     def w_far(layer, i):
         cols = pl.ds(pl.multiple_of(i * HALF, HALF), HALF)
         wst[i] = mm(ncol[:, cols], dab[...], 0, 0)
-        pltpu.make_async_copy(wst.at[i], WST.at[layer, cols], ls.at[S_ST + i]).start()
+        tail = jnp.logical_and(i == ONE, layer < TWO)
+
+        @pl.when(jnp.logical_not(tail))
+        def _():
+            pltpu.make_async_copy(wst.at[i], WST.at[layer, cols], ls.at[S_ST + i]).start()
+
+        for l, ref in enumerate((WT0, WT1)):
+            @pl.when(jnp.logical_and(i == ONE, layer == l))
+            def _():
+                pltpu.make_async_copy(wst.at[i], ref, ls.at[S_ST + i]).start()
 
     def w_send(layer, piece):
         p, k = home(layer)
@@ -902,9 +914,9 @@
 
     lax.fori_loop(0, NL, bwd_layer, 0)
 
-    w_sends(0, 0, NP + NP)
+    w_sends(0, 0, NP)
     w_sends(LAST, 13, 3)
-    w_sends(ONE, 1, 15)
+    w_sends(ONE, 1, 7)
     w_sends(TWO, 13, 3)
     grad_cols(0, d)
     x_sent(0)
@@ -965,11 +977,11 @@
             def _():
                 wait_for(WO.at[l], w_os.at[l, 0])
 
-        wait_for(WST.at[l], g_bs.at[l])
+        wait_for(WST.at[l] if l >= TWO else WST.at[l, pl.ds(0, HALF)], g_bs.at[l])
 
         @pl.when(c == p)
         def _():
-            wait_for(AB.at[0, pl.ds(0, 2)], g_b.at[l])
+            wait_for(AB.at[0, pl.ds(0, TWO if l >= TWO else ONE)], g_b.at[l])
             wait_for(AB.at[0, 0], g_c.at[l])
 
             @pl.when(al != p)
@@ -992,7 +1004,7 @@
             hbm((NM, 2, OWN, D), BF), hbm((2, MS, 4 * FS), F32), hbm((2, MS, 4 * FS), F32), hbm((2, FS, D), F32),
             hbm((NL, MS, F2C), BF), hbm((NL, FS // 2, D), BF),
             hbm((NL, D, F2C), BF), hbm((NL, FS, D), BF), hbm((NP, NM, ROWS, D), BF), hbm((NL, NM, ROWS, F2C), F32),
-            hbm((NS, NM, QUART, D), F32), hbm((NS, NM, OWN, D), F32), hbm((NL, MS, F2C), F32), hbm((NL, NM * ROWS, FS - SPLIT), BF), hbm((2, NM, OWN, D), BF),
+            hbm((NS, NM, QUART, D), F32), hbm((NS, NM, OWN, D), F32), hbm((NL, MS, F2C), F32), hbm((HALF, F2C), F32), hbm((HALF, F2C), F32), hbm((NL, NM * ROWS, FS - SPLIT), BF), hbm((2, NM, OWN, D), BF),
             hbm((LAST, NM * ROWS, F2C), BF), hbm((LAST, NM * ROWS, SPLIT), BF))
         scratch = [
             pltpu.VMEM((D, F2C), BF), pltpu.VMEM((FS, D), BF), pltpu.VMEM((ROWS, D), BF), pltpu.VMEM((ROWS, F2C), F32),
@@ -1007,7 +1019,53 @@
             kernel, out_shape=outs, in_specs=[any_spec] * 5, out_specs=(any_spec,) * len(outs), scratch_shapes=scratch,
             compiler_params=pltpu.CompilerParams(collective_id=0, has_side_effects=True, vmem_limit_bytes=67043328),
         )(x_loc.reshape(NM, 2, OWN, D), g_loc.reshape(NM, 2, OWN, D), gate_loc[0], in_loc[0], out_loc[0])
-        return res[0].reshape(x_loc.shape), res[1][None], res[2][None], res[3][None]
+        d_idx = lax.axis_index("data")
+        tails = []
+        for role_, val in ((0, res[OUT_T]), (ONE, res[OUT_T + ONE])):
+            for core in CORES:
+                pairs = [(TWO * q + core, TWO * ((q + TWO) % NL if role_ == 0 else q + ONE - TWO * (q % TWO))) for q in range(NL)]
+                tails.append(lax.ppermute(val, ("data", "stage"), pairs))
+        steps = 16
+        cost = pl.CostEstimate(flops=10 ** 11, bytes_accessed=10 ** 8, transcendentals=0)
+        blocks = [pl.BlockSpec((ONE, 2 * MS // steps, 4 * FS), lambda i: (i // (steps // TWO), i % (steps // TWO), 0))] * TWO
+        blocks.append(pl.BlockSpec((ONE, 2 * FS // steps, D), lambda i: (i // (steps // TWO), i % (steps // TWO), 0)))
+
+        def copy(*refs):
+            for src, dst in zip(refs[:LAST], refs[LAST:]):
+                dst[...] = src[...]
+
+        grads = pl.pallas_call(
+            copy, grid=(steps,), out_shape=tuple(hbm(v.shape, F32) for v in res[ONE:NL]), in_specs=blocks, out_specs=tuple(blocks),
+            cost_estimate=cost, compiler_params=pltpu.CompilerParams(vmem_limit_bytes=2 ** 25))(*res[ONE:NL])
+
+        def insert(t0, t1, t2, t3, gate_in, in_in, gate_out, in_out, buf, sems):
+            d = lax.axis_index("data")
+
+            @pl.when(lax.axis_index("stage") == 0)
+            def _():
+                loads, stores = [], []
+                for q, ref in enumerate((t0, t1, t2, t3)):
+                    k, core = home(q)
+                    far = d + TWO - NL * (d // TWO) if k == 0 else d + ONE - TWO * (d % TWO)
+                    col = (TWO * (far // TWO) + core) if k == 0 else (TWO * core + far % TWO)
+                    cols = pl.ds(pl.multiple_of(col * FS, QUART), FS)
+                    loads.append(pltpu.make_async_copy(ref, buf.at[q], sems.at[q]))
+                    for wi, out in enumerate((gate_out, in_out)):
+                        stores.append(pltpu.make_async_copy(buf.at[q, :, pl.ds(wi * FS, FS)], out.at[k, pl.ds(HALF, HALF), cols], sems.at[NL + TWO * q + wi]))
+                for cp in loads:
+                    cp.start()
+                for q in range(NL):
+                    loads[q].wait()
+                    for wi in CORES:
+                        stores[TWO * q + wi].start()
+                for cp in stores:
+                    cp.wait()
+
+        gate_g, in_g = pl.pallas_call(
+            insert, out_shape=tuple(hbm(v.shape, F32) for v in grads[:TWO]), in_specs=[any_spec] * (NL + TWO), out_specs=(any_spec,) * TWO,
+            scratch_shapes=[pltpu.VMEM((NL, HALF, F2C), F32), dma((NL + NP,))], input_output_aliases={NL: 0, NL + ONE: ONE},
+            compiler_params=pltpu.CompilerParams(vmem_limit_bytes=2 ** 25))(*tails, grads[0], grads[ONE])
+        return res[0].reshape(x_loc.shape), gate_g[None], in_g[None], grads[TWO][None]
 
     act_spec = P(None, "data", None, None)
     weight_spec = P("stage", None, "data", None)

time: 1300 us -> 1260 us (0.969)
  local copies, waits for them, and re-layouts: 48.7 us -> 1.33 us
  waiting for transfers between devices: 0 us -> 15.8 us
    pallas_call x1, Pallas kernels: 1240 us -> 1180 us  [body(): pl.pallas_call(kernel, out_shape=outs, in_specs=[any_spec] * 5, out_specs...]
    pallas_call x0 -> x2, Pallas kernels: none -> 51 us  [the longest x1 45.9 us: body(): pl.pallas_call(copy, grid=(steps,), out_shape=tuple((hbm(v.shape, F32) fo...]
    unnamed x16 -> x3, local copies, waits for them, and re-layouts: 48.7 us -> 1.33 us
    ppermute x0 -> x4, waiting for transfers between devices: none -> 15.8 us  [body(): tails.append(lax.ppermute(val, ('data', 'stage'), pairs))]
  transfers between devices with their start and end apart: 0 -> 4, of which waited for: 0 -> 4; matrix products, arithmetic and copies ran while one was open for 0% -> 0% of each run, Pallas kernels for 0% -> 4%
where the time goes in v5:
time: 1260 us
  Pallas kernels  1230 us (98%)
  waiting for transfers between devices  15.8 us (1%)
    pallas_call x1, Pallas kernels, body(): pl.pallas_call(kernel, out_shape=outs, in_specs=[any_spec] * 5, out_specs...  1180 us
    pallas_call x1, Pallas kernels, body(): pl.pallas_call(copy, grid=(steps,), out_shape=tuple((hbm(v.shape, F32) fo...  45.9 us
  transfers between devices with their start and end apart: 4, of which 4 were waited for; matrix products, arithmetic and copies ran while one was open for 0% of the time, Pallas kernels for 4%

profile of v5, /device:TPU:0, one launch (start us, length us, event | category | flops | bytes accessed | tf_op | source)
XLA Modules:
  0.0 1260.0 jit_solution(8073130742409187236)
XLA Ops:
  0.6 1182.9 %shard_map.84 = (bf16[4,2,64,2048]{3,2,1,0:T(8,128)(2,1)}, f32[2,512,5632]{2,1,0:T(8,128)}, f32[2,512,5632]{2,1,0:T(8,128)}, f32[2,1408,2048]{2,1,0:T(8,128)}, b...) custom-call(bf16[4,2,64,2048]{3,2,1,0:T(8,128)(2,1)} %bitcast.14, ...), custom_call_target="tpu_custom_call" | custom-call | tf_op jit(solution)/shard_map/pallas_call | solution.py:1018
  1183.5 1.3 collective-permute-start.1
  1184.8 2.0 collective-permute-start
  1186.8 1.3 collective-permute-start.3
  1188.1 3.6 collective-permute-start.2
  1191.7 45.9 %shard_map.85 = (f32[2,512,5632]{2,1,0:T(8,128)}, f32[2,512,5632]{2,1,0:T(8,128)}, f32[2,1408,2048]{2,1,0:T(8,128)}) custom-call(f32[2,512,5632]{2,1,0:T(8,128)} %get-tuple-element.18.refs_0_, f32[2,512,5632]{2,1,0:T(8,128)} %get-tuple-element.19.refs_1_, f32[2,1408,2048]{2,1,0:T(8,128)} %get-tuple-element.20.refs_2_), custom_call_target="tpu_custom_call" | custom-call | flops 99999997952 | bytes 100000000 | tf_op jit(solution)/shard_map/pallas_call | solution.py:1037
  1237.7 10.7 collective-permute-done.1.t1
  1248.4 1.9 collective-permute-done.t0
  1250.2 1.4 collective-permute-done.3.t3
  1251.6 1.9 collective-permute-done.2.t2
  1253.5 0.0 copy-start
  1253.5 5.1 shard_map.86
  1258.7 0.0 copy-done
  1258.7 1.3 copy.14
Async XLA Ops:
  1183.5 64.8 %collective-permute-start.1 = (f32[256,2816]{1,0:T(8,128)}, f32[256,2816]{1,0:T(8,128)S(1)}, u32[]{:S(2)}, u32[]{:S(2)}) collective-permute-start(f32[256,2816]{1,0:T(8,128)} %get-tuple-element.16), channel_id=1, source_target_pairs={{1,4},{3,6},{5,0},{7,2}} | collective-permute-start | bytes 8650760 | tf_op jit(solution)/shard_map/ppermute | solution.py:1027
  1184.8 65.4 %collective-permute-start = (f32[256,2816]{1,0:T(8,128)}, f32[256,2816]{1,0:T(8,128)S(1)}, u32[]{:S(2)}, u32[]{:S(2)}) collective-permute-start(f32[256,2816]{1,0:T(8,128)} %get-tuple-element.16), channel_id=1, source_target_pairs={{0,4},{2,6},{4,0},{6,2}} | collective-permute-start | bytes 8650760 | tf_op jit(solution)/shard_map/ppermute | solution.py:1027
  1186.8 64.8 %collective-permute-start.3 = (f32[256,2816]{1,0:T(8,128)}, f32[256,2816]{1,0:T(8,128)S(1)}, u32[]{:S(2)}, u32[]{:S(2)}) collective-permute-start(f32[256,2816]{1,0:T(8,128)} %get-tuple-element.17), channel_id=1, source_target_pairs={{1,2},{3,0},{5,6},{7,4}} | collective-permute-start | bytes 8650760 | tf_op jit(solution)/shard_map/ppermute | solution.py:1027
  1188.1 65.4 %collective-permute-start.2 = (f32[256,2816]{1,0:T(8,128)}, f32[256,2816]{1,0:T(8,128)S(1)}, u32[]{:S(2)}, u32[]{:S(2)}) collective-permute-start(f32[256,2816]{1,0:T(8,128)} %get-tuple-element.17), channel_id=1, source_target_pairs={{0,2},{2,0},{4,6},{6,4}} | collective-permute-start | bytes 8650760 | tf_op jit(solution)/shard_map/ppermute | solution.py:1027
  1253.5 5.1 copy-start
